TPU v7x, 256 devices: a whole 4x4x8 slice. The times are simulated.
256 devices in a mesh: dp: 32 (over x, y, core), tensor: 8 (over z).
Axes of the slice: x: 4, y: 4, z: 8, core: 2. Of those that a mesh axis runs over, the one named last changes fastest.
Arguments:
- proxy_hidden: bfloat16 [1536, 4096], P('dp', 'tensor'), may hold values from -176.625 to 176.625
- reference_hidden: bfloat16 [1536, 4096], P('dp', 'tensor'), may hold values from -176.625 to 176.625
- proxy_head: bfloat16 [128256, 4096], P(('dp', 'tensor')), may hold values from -0.09375 to 0.09375
- reference_head: bfloat16 [128256, 4096], P(('dp', 'tensor')), may hold values from -0.09375 to 0.09375
- targets: int32 [1536], P('dp'), may hold values from 0 to 128255
- domains: int32 [1536], P('dp'), may hold values from 0 to 127
- keep_mask: int32 [1536], P('dp'), may hold values 0 or 1
- prior_weights: float32 [128], replicated, may hold values from 0.5 to 2
Outputs:
- excess: float32 [1536], P('dp')
- log_weights: float32 [128], replicated
All inputs are finite; a program needn't handle non-finite values. No bound on the sum of `keep_mask` on one device may be relied on, other than what follows from the above.
Results may differ from a plain program's by a relative error of at most 0.00045.
Values may be sent and summed in bfloat16 or wider, within the bound.
A program may use at most 128 MiB of HBM per device.

v0:
```python
import jax
import jax.numpy as jnp
from jax import lax
from jax.sharding import Mesh
from jax.sharding import PartitionSpec as P

DOMAINS = 128
STEPS = 3
DP = ("dp_0", "dp_1", "dp_2")
DP_TENSOR = ("dp_0", "dp_1", "dp_2", "tensor")


step_size = 1.0
smoothing = 0.001


def gather_turned(arrays, axis, dims):
    turned = [jnp.moveaxis(a, dim, 0) for a, dim in zip(arrays, dims)]
    widths = [t[0].size for t in turned]
    both = jnp.concatenate([t.reshape(-1, w) for t, w in zip(turned, widths)], axis=1)
    whole = lax.all_gather(both, axis, axis=0, tiled=True)
    pieces = jnp.split(whole, [sum(widths[:k]) for k in range(1, len(widths))], axis=1)
    return tuple(
        (
            jnp.moveaxis(b.reshape(-1, *t.shape[1:]), 0, dim)
            for b, t, dim in zip(pieces, turned, dims)
        )
    )


def copy_for_each(array, axis):
    copies = jnp.broadcast_to(array, (lax.axis_size(axis), *array.shape))
    return lax.all_to_all(copies, axis, split_axis=0, concat_axis=0, tiled=True)


def in_order(pieces, dim):
    dims = list(pieces.shape[1:])
    dims[dim] *= pieces.shape[0]
    return jnp.moveaxis(pieces, 0, dim).reshape(dims)


def gather_directly(array, axis, dim):
    pieces = copy_for_each(array, axis)
    return in_order(pieces, dim)


def all_in_one(array, axis):
    leaves = jax.tree.leaves(array)
    turns = sorted(range(len(leaves)), key=lambda k: -leaves[k].size)
    width = (1, *leaves[turns[0]].shape)[-1]
    lines = [
        jnp.pad(leaves[k].reshape(-1), (0, -leaves[k].size % width)).reshape(-1, width)
        for k in turns
    ]
    both, at, found = (lax.all_gather(jnp.concatenate(lines), axis), 0, {})
    for k, line in zip(turns, lines):
        share = both[:, at : at + len(line)].reshape(len(both), -1)
        found[k] = share[:, : leaves[k].size].reshape(-1, *leaves[k].shape)
        at += len(line)
    numbers = iter(range(len(leaves)))
    return jax.tree.map(lambda _: found[next(numbers)], array)


def combined_by_axis(array, axes, combine):
    for axis in axes:
        pieces = all_in_one(array, axis)
        array = jax.tree.map(lambda part: part[0], pieces)
        for k in range(1, lax.axis_size(axis)):
            array = combine(array, jax.tree.map(lambda part: part[k], pieces))
    return array


def project(rows, head):
    return lax.dot_general(rows, head, (((1,), (1,)), ((), ())), preferred_element_type=jnp.float32)


def row_stats(logits, wanted):
    columns = jnp.arange(logits.shape[1], dtype=jnp.int32)
    row_peak = jnp.max(logits, axis=1)
    row_total = jnp.sum(jnp.exp(logits - row_peak[:, None]), axis=1)
    matched = wanted[:, None] == columns[None, :]
    row_hit = jnp.sum(jnp.where(matched, logits, 0.0), axis=1)
    return jnp.stack([row_peak, row_total, row_hit])


def update_weights(prior_weights, clipped, domains, keep):
    weights = prior_weights / jnp.sum(prior_weights)
    batch_rows = clipped.shape[0] // STEPS
    labels = jnp.arange(DOMAINS, dtype=jnp.int32)
    for section_index in range(STEPS):
        row_start = section_index * batch_rows
        block_loss = clipped[row_start : row_start + batch_rows]
        block_keep = keep[row_start : row_start + batch_rows]
        member = (domains[row_start : row_start + batch_rows][:, None] == labels[None, :]).astype(
            jnp.float32
        )
        domain_sum = jnp.dot(block_loss, member, precision=lax.Precision.HIGHEST)
        domain_count = jnp.dot(block_keep, member, precision=lax.Precision.HIGHEST)
        domain_gain = domain_sum / jnp.maximum(domain_count, 1.0)
        raised = weights * jnp.exp(step_size * domain_gain)
        weights = (1.0 - smoothing) * raised / jnp.sum(raised) + smoothing / DOMAINS
    return jnp.log(weights)


def merge_stats(earlier_part, second_part):
    peak_one, total_one, hit_one = earlier_part
    peak_two, total_two, hit_two = second_part
    top_value = jnp.maximum(peak_one, peak_two)
    joined = total_one * jnp.exp(peak_one - top_value) + total_two * jnp.exp(peak_two - top_value)
    return (top_value, joined, hit_one + hit_two)


def local(
    proxy_hidden,
    reference_hidden,
    proxy_head,
    reference_head,
    targets,
    domains,
    keep_mask,
    prior_weights,
):
    all_targets, all_domains, all_keep = gather_turned((targets, domains, keep_mask), DP, (0, 0, 0))
    vocab_dev = proxy_head.shape[0]
    offset = (lax.axis_index(DP) * lax.axis_size("tensor") + lax.axis_index("tensor")) * vocab_dev
    local_target = all_targets - offset
    stacked = jnp.stack([proxy_hidden, reference_hidden])
    full_rows = gather_directly(stacked, "tensor", 2)
    portion = lax.all_gather(full_rows, DP, axis=1, tiled=True)
    proxy_part = row_stats(project(portion[0], proxy_head), local_target)
    reference_part = row_stats(project(portion[1], reference_head), local_target)
    stats = jnp.concatenate([proxy_part, reference_part], axis=0)
    local_peaks = jnp.stack([stats[0], stats[3]])
    local_totals = jnp.stack([stats[1], stats[4]])
    local_hits = jnp.stack([stats[2], stats[5]])
    global_peak, totals, hit_sum = combined_by_axis(
        (local_peaks, local_totals, local_hits), DP_TENSOR, merge_stats
    )
    losses = global_peak + jnp.log(totals) - hit_sum
    keep = all_keep.astype(jnp.float32)
    loss_gap = losses[0] - losses[1]
    excess_all = loss_gap * keep
    clipped = jnp.maximum(loss_gap, 0.0) * keep
    log_weights = update_weights(prior_weights, clipped, all_domains, keep)
    tok_dev = targets.shape[0]
    mine = lax.dynamic_slice_in_dim(excess_all, lax.axis_index(DP) * tok_dev, tok_dev, 0)
    return (mine, log_weights)


def solution(mesh):
    split = Mesh(
        mesh.devices.reshape(4, 4, 2, mesh.shape["tensor"]), ("dp_0", "dp_1", "dp_2", "tensor")
    )
    return jax.shard_map(
        local,
        mesh=split,
        in_specs=(
            P(DP, "tensor"),
            P(DP, "tensor"),
            P(DP_TENSOR, None),
            P(DP_TENSOR, None),
            P(DP),
            P(DP),
            P(DP),
            P(),
        ),
        out_specs=(P(DP), P()),
        check_vma=False,
    )
```

profile of v0, /device:TPU:2, one launch (start us, length us, event | category | flops | bytes accessed | tf_op | source)
XLA Modules:
  0.0 223.1 jit_solution(5851774989392335685)
XLA Ops:
  7.2 0.0 copy-start
  7.2 0.0 copy-start.1
  7.2 0.0 copy-start.2
  7.2 0.0 copy-start.4
  7.2 0.0 all-gather.11.cloned.1.call-start
  7.3 0.8 pad_maximum_fusion
  8.1 0.1 broadcast_in_dim.7
  8.2 31.4 %all_to_all.5 = bf16[8,2,48,512]{3,2,1,0:T(8,128)(2,1)S(1)} all-to-all(bf16[8,2,48,512]{3,2,1,0:T(8,128)(2,1)S(1)} %broadcast_in_dim.7), channel_id=1, replica_groups=mesh['dp_0'=4,'dp_1'=4,'dp_2'=2,'tensor'=8] {'tensor'}, dimensions={0} | all-to-all | bytes 1572864 | tf_op jit(solution)/shard_map/all_to_all | solution.py:33
  39.5 1.0 copy.13
  40.6 0.0 all-gather.11.cloned.1.call-update
  40.6 0.0 copy-done
  40.6 0.0 copy-done.1
  40.6 0.0 copy-done.2
  40.6 24.7 %all-gather.4 = s32[32,48,3]{1,2,0:T(4,128)S(1)} all-gather(s32[1,48,3]{1,2,0:T(4,128)S(1)} %add_bitcast_fusion), channel_id=1, replica_groups=mesh['dp_0'=4,'dp_1'=4,'dp_2'=2,'tensor'=8] {'dp_0','dp_1','dp_2'}, dimensions={0}, use_global_device_ids=true | all-gather | bytes 19008 | tf_op jit(solution)/shard_map/all_gather | solution.py:21
  65.3 0.1 reshape.79
  65.5 0.0 copy-done.4
  65.5 0.6 reduce_sum.76
  66.1 0.3 fusion.9
  66.4 0.3 fusion.5
  66.7 0.3 fusion.13
  67.0 67.0 %all-gather.11.cloned.1.call-done = bf16[2,1536,4096]{2,1,0:T(8,128)(2,1)} async-done(((bf16[2,48,4096]{2,1,0:T(8,128)(2,1)}), bf16[2,1536,4096]{2,1,0:T(8,128)(2,1)}) %all-gather.11.cloned.1.call-update) | async-done | bytes 25165840 | tf_op jit(solution)/shard_map/all_gather | solution.py:129
  134.0 0.0 copy-start.3
  134.0 10.6 %fusion.94 = (f32[1536]{0:T(1024)S(1)}, f32[1536,501]{0,1:T(8,128)S(1)}) fusion(bf16[501,4096]{1,0:T(8,128)(2,1)} %param.10, bf16[2,1536,4096]{2,1,0:T(8,128)(2,1)} %all-gather.11.cloned.1.call-done), kind=kOutput, calls=%fused_computation.175 | convolution fusion | flops 6304806912 | bytes 19795968 | tf_op jit(solution)/shard_map/dot_general | solution.py:74
  144.7 0.0 copy-done.3
  144.7 9.7 %fusion.95 = (f32[1536]{0:T(1024)S(1)}, f32[1536,501]{0,1:T(8,128)S(1)}) fusion(bf16[501,4096]{1,0:T(8,128)(2,1)S(1)} %copy-done.3, bf16[2,1536,4096]{2,1,0:T(8,128)(2,1)} %all-gather.11.cloned.1.call-done), kind=kOutput, calls=%fused_computation.176 | convolution fusion | flops 6304806912 | bytes 19771392 | tf_op jit(solution)/shard_map/dot_general | solution.py:74
  154.4 1.5 select_reduce_fusion
  155.9 0.1 concatenate.17
  156.0 12.4 %all-gather.5 = f32[4,6,1536]{2,1,0:T(8,128)S(1)} all-gather(f32[1,6,1536]{2,1,0:T(8,128)S(1)} %bitcast.371), channel_id=2, replica_groups=mesh['dp_0'=4,'dp_1'=4,'dp_2'=2,'tensor'=8] {'dp_0'}, dimensions={0}, use_global_device_ids=true | all-gather | bytes 184320 | tf_op jit(solution)/shard_map/all_gather | solution.py:55
  168.4 0.1 fusion.61
  168.5 12.1 %all-gather.6 = f32[4,6,1536]{2,1,0:T(8,128)S(1)} all-gather(f32[1,6,1536]{2,1,0:T(8,128)S(1)} %maximum_bitcast_fusion), channel_id=3, replica_groups=mesh['dp_0'=4,'dp_1'=4,'dp_2'=2,'tensor'=8] {'dp_1'}, dimensions={0}, use_global_device_ids=true | all-gather | bytes 184320 | tf_op jit(solution)/shard_map/all_gather | solution.py:55
  180.7 0.1 fusion.51
  180.8 1.9 all-gather.7
  182.7 26.7 %all-gather.8 = f32[8,6,1536]{2,1,0:T(8,128)S(1)} all-gather(f32[1,6,1536]{2,1,0:T(8,128)S(1)} %maximum_bitcast_fusion.2), channel_id=5, replica_groups=mesh['dp_0'=4,'dp_1'=4,'dp_2'=2,'tensor'=8] {'tensor'}, dimensions={0}, use_global_device_ids=true | all-gather | bytes 331776 | tf_op jit(solution)/shard_map/all_gather | solution.py:55
  209.4 0.2 fusion.21
  209.7 0.6 dynamic-slice_multiply_fusion
  210.3 1.6 fusion.96
  211.9 1.6 fusion.97
  213.5 1.6 fusion.98
  215.1 1.2 add_log_fusion
  (21 shorter events, 0.3 us)
Async XLA Ops:
  7.2 33.4 %copy-start = (s32[48]{0:T(128)S(1)}, s32[48]{0:T(128)}, u32[]{:S(2)}) copy-start(s32[48]{0:T(128)} %param.14) | copy-start | bytes 580
  7.2 33.4 %copy-start.1 = (s32[48]{0:T(128)S(1)}, s32[48]{0:T(128)}, u32[]{:S(2)}) copy-start(s32[48]{0:T(128)} %param.13) | copy-start | bytes 580
  7.2 33.4 %copy-start.2 = (s32[48]{0:T(128)S(1)}, s32[48]{0:T(128)}, u32[]{:S(2)}) copy-start(s32[48]{0:T(128)} %param.12) | copy-start | bytes 580
  7.2 58.3 %copy-start.4 = (f32[128]{0:T(128)S(1)}, f32[128]{0:T(128)}, u32[]{:S(2)}) copy-start(f32[128]{0:T(128)} %param.15) | copy-start | bytes 1540
  7.2 126.8 %all-gather.11.cloned.1.call-start = ((), (), s32[]{:S(2)}) async-start(), calls=%async_computation.1 | async-start | bytes 25952256 | tf_op jit(solution)/shard_map/all_gather | solution.py:129
  134.0 10.7 %copy-start.3 = (bf16[501,4096]{1,0:T(8,128)(2,1)S(1)}, bf16[501,4096]{1,0:T(8,128)(2,1)}, u32[]{:S(2)}) copy-start(bf16[501,4096]{1,0:T(8,128)(2,1)} %param.11) | copy-start | bytes 12312580
Sparse Core Ops, SparseCore 0:
  40.7 93.2 all-gather.10
where the time goes:
time: 223 us
  blocking collectives  109 us (49%)
  waiting for transfers between devices  67 us (30%)
  matrix products  26 us (12%)
  between operations  14.3 us (6%)
  other arithmetic  5.31 us (2%)
    all_gather x1, waiting for transfers between devices, local(): portion = lax.all_gather(full_rows, DP, axis=1, tiled=True)  67 us
    all_gather x4, blocking collectives, all_in_one(): both, at, found = (lax.all_gather(jnp.concatenate(lines), axis), 0, {})  53.1 us
    all_to_all x1, blocking collectives, copy_for_each(): return lax.all_to_all(copies, axis, split_axis=0, concat_axis=0, tiled=True)  31.4 us
    all_gather x1, blocking collectives, gather_turned(): whole = lax.all_gather(both, axis, axis=0, tiled=True)  24.7 us
    dot_general x2, matrix products, project(): lax.dot_general(rows, head, (((1,), (1,)), ((), ())), preferred_element_t...  20.3 us
    dot_general x3, matrix products, update_weights(): domain_sum = jnp.dot(block_loss, member, precision=lax.Precision.HIGHEST)  4.82 us
  transfers between devices with their start and end apart: 1, of which 1 were waited for; matrix products, arithmetic and copies ran while one was open for 1% of the time, Pallas kernels for 0%

commit v1 on v0

v1 whole, which is shorter than its diff:
```python
import jax
import jax.numpy as jnp
from jax import lax
from jax.experimental import pallas as pl
from jax.experimental.pallas import tpu as pltpu
from jax.sharding import Mesh
from jax.sharding import PartitionSpec as P

DOMAINS = 128
STEPS = 3
DP = ("dp_0", "dp_1", "dp_2")
DP_TENSOR = ("dp_0", "dp_1", "dp_2", "tensor")
AXIS = {"x": "dp_0", "y": "dp_1", "z": "tensor"}
MESH = pl.DeviceIdType.MESH

step_size = 1.0
smoothing = 0.001

KB = 1024
RATE = 46.6e3
HOP = 2.4
START = 2.0
LEAD = 3.0
RING4 = (0, 1, -1, 2)
RING8 = (0, 1, -1, 2, -2, 3, -3, 4)


def ring(add, axis, size, token, deps, far, rank):
    for k in range(1, far + 1):
        half = (0, 1) if k == far else (None, None)
        part = size // 2 if k == far else size
        for sign, h in ((1, half[0]), (-1, half[1])):
            source = token(-sign * (k - 1), h)
            given = token(far if k == far else -sign * k, h)
            need = deps if k == 1 else [token(-sign * (k - 1), None)]
            add(axis, sign, part, source, need, given, rank + 0.01 * k)


def gather_plan():
    copies = []

    def add(axis, sign, size, source, need, given, rank):
        copies.append(
            dict(axis=axis, sign=sign, size=size, source=source, need=need, given=given, rank=rank)
        )

    piece = 32 * KB
    for colour, first, last in (("A", "y", "x"), ("B", "x", "y")):
        ring(add, "z", piece, lambda d, h: (colour, "z", d, h), [(colour, "z", 0, None)], 4, 0)
        for dz in RING8:
            have = [(colour, "z", dz, None)]
            ring(add, first, piece, lambda d, h: (colour, "f", dz, d, h), have, 2, 1)
            full = have + [(colour, "f", dz, d, None) for d in (1, -1, 2)]
            ring(add, last, 4 * piece, lambda d, h: (colour, "l", dz, d, h), full, 2, 3)
    piece = 16 * KB
    for colour, first, last in (("C0", "x", "y"), ("C1", "y", "x")):
        own = [(colour, "f", 0, None)]
        ring(add, first, piece, lambda d, h: (colour, "f", d, h), own, 2, 0)
        full = own + [(colour, "f", d, None) for d in (1, -1, 2)]
        ring(add, last, 4 * piece, lambda d, h: (colour, "l", d, h), full, 2, 0)
        for j in RING4:
            have = full if j == 0 else [(colour, "l", j, None)]
            ring(add, "z", 4 * piece, lambda d, h: (colour, "z", j, d, h), have, 4, 2)
    return copies


def parts_of(token, known):
    if token in known:
        return [token]
    return [token[:-1] + (0,), token[:-1] + (1,)]


OWN = {("A", "z", 0, None), ("B", "z", 0, None), ("C0", "f", 0, None), ("C1", "f", 0, None)}


def schedule(copies, computes):
    known = {c["given"] for c in copies} | OWN
    for c in copies:
        c["deps"] = [p for t in c["need"] for p in parts_of(t, known)]
    have = {t: START for t in OWN}
    free = {}
    waiting = list(range(len(copies)))
    while waiting:
        best = None
        for i in waiting:
            c = copies[i]
            if all(d in have for d in c["deps"]):
                ready = max(have[d] for d in c["deps"])
                link = (c["axis"], c["sign"])
                begin = max(ready, free.get(link, START))
                key = (begin, c["rank"], ready, i)
                if best is None or key < best:
                    best = key
        begin, _, ready, i = best
        c = copies[i]
        c["start"], c["ready"] = begin, ready
        free[(c["axis"], c["sign"])] = begin + c["size"] / RATE
        have[c["given"]] = begin + c["size"] / RATE + HOP
        waiting.remove(i)
    events = []
    for i, c in enumerate(copies):
        events.append((have[c["given"]], 0, i, "recv"))
        events.append((max(c["ready"], c["start"] - LEAD), 1, i, "send"))
    for i, (_, tokens) in enumerate(computes):
        when = max(have[p] for t in tokens for p in parts_of(t, known))
        events.append((when, 2, i, "compute"))
    return [(kind, i) for _, _, i, kind in sorted(events)]


def group_tokens(group, dzs):
    out = []
    for dz in dzs:
        if group == "C":
            for colour in ("C0", "C1"):
                for j in RING4:
                    if dz != 0:
                        out.append((colour, "z", j, dz, None))
                    elif j != 0:
                        out += [(colour, "l", j, None), (colour, "f", j, None)]
        else:
            for colour in ("A", "B"):
                if group == 0:
                    out += [(colour, "z", dz, None)]
                    out += [(colour, "f", dz, d, None) for d in (1, -1, 2)]
                elif group == 1:
                    out += [(colour, "l", dz, d, None) for d in (1, -1)]
                else:
                    out += [(colour, "l", dz, 2, None)]
    return out


WORK = [
    (0, (0, 1, -1)), (0, (2, -2)), (0, (3, -3, 4)),
    (1, (0, 1, -1)), (1, (2, -2)), (1, (3, -3, 4)),
    (2, (0, 1, -1)), (2, (2, -2)), (2, (3, -3)), (2, (4,)),
    ("C", (0, 1, -1)), ("C", (2, -2)), ("C", (3, -3)), ("C", (4,)),
]


def flat(x):
    return x.reshape(x.shape[0] * x.shape[1], x.shape[2]) if x.ndim == 3 else x


def kernel(
    copies, order, rows,
    ph, rh, pw, rw, meta_in, out,
    G, W, acc0, acc1, acc2, accC, M0, M1, st, zbuf, ybuf, xbuf, dbuf,
    own_sem, head_sem, swap_send, swap_recv, g_send, g_recv, m_send, m_recv, s_send, s_recv,
):
    x, y, c, z = (lax.axis_index(a) for a in ("dp_0", "dp_1", "dp_2", "tensor"))
    other = 1 - c
    pos = {"x": (x, 4), "y": (y, 4), "z": (z, 8)}

    def at(axis, d):
        p, n = pos[axis]
        return lax.rem(p + (d % n), n) if d % n else p

    def peer(axis, d):
        return {AXIS[axis]: at(axis, d)}

    def cols(dz, half=None):
        begin = at("z", dz) * 512
        if half is None:
            return pl.ds(pl.multiple_of(begin, 512), 512)
        return pl.ds(pl.multiple_of(begin + 256 * half, 256), 256)

    def view(token):
        colour, phase, half = token[0], token[1], token[-1]
        if colour in ("A", "B"):
            k = 0 if colour == "A" else 1
            last, first = ("x", "y") if colour == "A" else ("y", "x")
            ms = slice(0, 2) if half is None else half
            dz = token[2]
            if phase == "z":
                return G.at[k, ms, at(last, 0), at(first, 0), :, cols(dz)]
            if phase == "f":
                return G.at[k, ms, at(last, 0), at(first, token[3]), :, cols(dz)]
            return G.at[k, ms, at(last, token[3]), :, :, cols(dz)]
        d = token[2]
        if phase == "f":
            if colour == "C0":
                return G.at[2, 0, at("x", d), y, :, cols(0, half)]
            return G.at[2, 1, x, at("y", d), :, cols(0, half)]
        cs = cols(0 if phase == "l" else token[3], half)
        if colour == "C0":
            return G.at[2, 0, :, at("y", d), :, cs]
        return G.at[2, 1, at("x", d), :, :, cs]

    def gather_copy(i, token, sign):
        ref = view(token)
        return pltpu.make_async_remote_copy(
            src_ref=ref, dst_ref=ref, send_sem=g_send.at[i], recv_sem=g_recv.at[i],
            device_id=peer(copies[i]["axis"], sign), device_id_type=MESH,
        )

    own = []
    for m, src in enumerate((ph, rh)):
        for k in range(3):
            dst = G.at[k, m, y, x, :, cols(0)] if k == 1 else G.at[k, m, x, y, :, cols(0)]
            own.append(pltpu.make_async_copy(src.at[pl.ds(16 * k, 16), :], dst, own_sem.at[3 * m + k]))
    own.append(pltpu.make_async_copy(meta_in, M0.at[y], own_sem.at[6]))
    for copy in own:
        copy.start()
    heads = (pw, rw)
    mine = [pltpu.make_async_copy(heads[m], W.at[m, 0], head_sem.at[m]) for m in (0, 1)]
    for copy in mine:
        copy.start()

    barrier = pltpu.get_barrier_semaphore()
    peers = [peer("z", d) for d in range(1, 8)] + [peer(a, d) for a in "xy" for d in (1, 2, 3)]
    peers.append({"dp_2": other})
    for target in peers:
        pl.semaphore_signal(barrier, inc=1, device_id=target, device_id_type=MESH)
    st[...] = jnp.zeros_like(st)
    pl.semaphore_wait(barrier, len(peers))

    for copy in own:
        copy.wait()

    def meta_copy(i, axis, d, sending):
        slot = at(axis, 0 if sending else -d)
        src, dst = (M0.at[slot], M0.at[slot]) if axis == "y" else (M0, M1.at[slot])
        return pltpu.make_async_remote_copy(
            src_ref=src, dst_ref=dst, send_sem=m_send.at[i], recv_sem=m_recv.at[i],
            device_id=peer(axis, d), device_id_type=MESH,
        )

    for d in (1, 2, 3):
        meta_copy(d - 1, "y", d, True).start()

    def swap_copy(i, m, dz):
        return pltpu.make_async_remote_copy(
            src_ref=heads[m].at[:, cols(dz)], dst_ref=W.at[m, 1, :, cols(dz)],
            send_sem=swap_send.at[i], recv_sem=swap_recv.at[i],
            device_id={"dp_2": other}, device_id_type=MESH,
        )

    swaps = {(m, dz): (2 * q + m) for q, dz in enumerate(RING8) for m in (0, 1)}

    f32 = jnp.float32
    lane = lax.broadcasted_iota(jnp.int32, (8, 128), 1)
    sub = lax.broadcasted_iota(jnp.int32, (8, 128), 0)
    accs = {0: acc0, 1: acc1, 2: acc2, "C": accC}

    def block(group, m, dz):
        cs = cols(dz)
        if group == "C":
            return G[2, m, :, :, :, cs].reshape(256, 512)
        pieces = []
        for d in {0: (0,), 1: (-1, 1), 2: (2,)}[group]:
            pieces.append(G[0, m, at("x", d), :, :, cs].reshape(64, 512))
            pieces.append(G[1, m, at("y", d), :, :, cs].reshape(64, 512))
        return jnp.concatenate(pieces, axis=0)

    done_heads = set()

    def compute(i):
        group, dzs = WORK[i]
        if "own" not in done_heads:
            for copy in mine:
                copy.wait()
            done_heads.add("own")
        for dz in dzs:
            for m in (0, 1):
                if (m, dz) not in done_heads:
                    swap_copy(swaps[(m, dz)], m, dz).wait_recv()
                    done_heads.add((m, dz))
        acc = accs[group]
        first = 0 in dzs

        def body(m, carry):
            rhs = [block(group, m, dz) for dz in dzs]
            for h in (0, 1):
                total = None
                for dz, r in zip(dzs, rhs):
                    part = lax.dot_general(
                        W[m, h, :, cols(dz)], r, (((1,), (1,)), ((), ())), preferred_element_type=f32
                    )
                    total = part if total is None else total + part
                acc[m, h] = total if first else acc[m, h] + total
            return carry

        lax.fori_loop(0, 2, body, 0)

    dev = ((x * 4 + y) * 2 + c) * 8 + z
    dev_other = ((x * 4 + y) * 2 + other) * 8 + z
    offsets = (dev * rows, dev_other * rows)

    def spread(quantity):
        j = lax.broadcasted_iota(jnp.int32, (128, 128), 0)
        l = lax.broadcasted_iota(jnp.int32, (128, 128), 1)
        low = l % 16
        sel_ab = (j == low + jnp.where(l < 64, 0, 16)).astype(f32)
        sel_c = (j == low + 32).astype(f32)
        ab = jnp.dot(quantity, sel_ab, precision=lax.Precision.HIGHEST, preferred_element_type=f32)
        cc = jnp.dot(quantity, sel_c, precision=lax.Precision.HIGHEST, preferred_element_type=f32)
        d = lax.broadcasted_iota(jnp.int32, (16, 128), 0)
        l = lax.broadcasted_iota(jnp.int32, (16, 128), 1)
        q = (l // 16) % 4
        result = jnp.zeros((8, 128), f32)
        for a in range(4):
            owner = jnp.where(l < 64, a * 4 + q, q * 4 + a)
            row = jnp.sum(jnp.where(d == owner, ab, 0.0), axis=0, keepdims=True)
            result = jnp.where(sub == a, row, result)
        for a in range(2):
            owner = (2 * a + l // 64) * 4 + q
            row = jnp.sum(jnp.where(d == owner, cc, 0.0), axis=0, keepdims=True)
            result = jnp.where(sub == 4 + a, row, result)
        return result

    def stats(group, wanted):
        acc = accs[group]
        width = acc.shape[-1]
        if group == "C":
            places = [sub == 4, sub == 5]
        else:
            places = [
                sub == jnp.where(lane < 64, at("x", d), at("y", d))
                for d in {0: (0,), 1: (-1, 1), 2: (2,)}[group]
            ]
        want = [jnp.sum(jnp.where(p, wanted, 0.0), axis=0, keepdims=True) for p in places]
        want = jnp.concatenate(want, axis=1).astype(jnp.int32) if len(want) > 1 else want[0].astype(jnp.int32)
        vocab = lax.broadcasted_iota(jnp.int32, (rows, width), 0)
        lses, hits = [], []
        for m in (0, 1):
            peak = jnp.maximum(
                jnp.max(acc[m, 0], axis=0, keepdims=True), jnp.max(acc[m, 1], axis=0, keepdims=True)
            )
            total = jnp.zeros((1, width), f32)
            hit = jnp.zeros((1, width), f32)
            for h in (0, 1):
                logits = acc[m, h]
                total += jnp.sum(jnp.exp(logits - peak), axis=0, keepdims=True)
                match = vocab == want - offsets[h]
                hit += jnp.sum(jnp.where(match, logits, 0.0), axis=0, keepdims=True)
            lses.append(peak + jnp.log(total))
            hits.append(hit)
        for k, row in enumerate((lses[0], lses[1], hits[0] - hits[1])):
            value = st[k]
            for b, place in enumerate(places):
                value = jnp.where(place, row[:, 128 * b : 128 * (b + 1)], value)
            st[k] = value

    started_swaps = False
    meta_done = False
    tables = {}
    pending = {g: sum(1 for w in WORK if w[0] == g) for g in accs}
    for kind, i in order:
        if kind == "send":
            gather_copy(i, copies[i]["source"], copies[i]["sign"]).start()
        elif kind == "recv":
            if not started_swaps:
                for (m, dz), s in swaps.items():
                    swap_copy(s, m, dz).start()
                started_swaps = True
            gather_copy(i, copies[i]["given"], copies[i]["sign"]).wait_recv()
        else:
            if not meta_done:
                meta_done = True
                for d in (1, 2, 3):
                    meta_copy(d - 1, "y", d, False).wait_recv()
                M1[x] = M0[...]
                for d in (1, 2, 3):
                    meta_copy(2 + d, "x", d, True).start()
            compute(i)
            group = WORK[i][0]
            pending[group] -= 1
            if not pending[group]:
                if not tables:
                    for d in (1, 2, 3):
                        meta_copy(2 + d, "x", d, False).wait_recv()
                    for k, name in enumerate(("targets", "domains", "keep")):
                        tables[name] = spread(M1[:, :, k, :].reshape(16, 128))
                stats(group, tables["targets"])

    def exchange(buf, axis, base):
        n = pos[axis][1]

        def copy(d, slot):
            return pltpu.make_async_remote_copy(
                src_ref=buf.at[slot], dst_ref=buf.at[slot],
                send_sem=s_send.at[base + d - 1], recv_sem=s_recv.at[base + d - 1],
                device_id=peer(axis, d), device_id_type=MESH,
            )

        for d in range(1, n):
            copy(d, at(axis, 0)).start()
        for d in range(1, n):
            copy(d, at(axis, -d)).wait_recv()
        parts = [[buf[s, k] for k in range(3)] for s in range(n)]
        combined = []
        for k in (0, 1):
            peak = parts[0][k]
            for s in range(1, n):
                peak = jnp.maximum(peak, parts[s][k])
            total = jnp.exp(parts[0][k] - peak)
            for s in range(1, n):
                total = total + jnp.exp(parts[s][k] - peak)
            combined.append(peak + jnp.log(total))
        hit = parts[0][2]
        for s in range(1, n):
            hit = hit + parts[s][2]
        combined.append(hit)
        return combined, [copy(d, at(axis, 0)) for d in range(1, n)]

    zbuf[z] = st[...]
    result, sent_z = exchange(zbuf, "z", 0)
    for k in range(3):
        ybuf[y, k] = result[k]
    result, sent_y = exchange(ybuf, "y", 7)
    for k in range(3):
        xbuf[x, k] = result[k]
    (lse0, lse1, hit), sent_x = exchange(xbuf, "x", 10)

    keep = tables["keep"]
    gap = (lse0 - lse1) - hit
    excess = gap * keep
    clipped = jnp.maximum(gap, 0.0) * keep
    q = (lane // 16) % 4
    low = lane % 16
    owner = jnp.where(sub < 4, jnp.where(lane < 64, sub * 4 + q, q * 4 + sub), (2 * (sub - 4) + lane // 64) * 4 + q)
    colour = jnp.where(sub < 4, jnp.where(lane < 64, 0, 1), 2)
    token = (owner * 2 + c) * 48 + 16 * colour + low
    batch = token // 512
    label = lax.broadcasted_iota(jnp.int32, (128, 128), 0).astype(f32)
    left, right = [], []
    for b in range(6):
        bb = batch[b : b + 1, :]
        top = jnp.where(bb == sub, clipped[b : b + 1, :], 0.0)
        low_rows = jnp.where(bb == sub - 3, keep[b : b + 1, :], 0.0)
        left.append(jnp.where(sub < 3, top, low_rows))
        right.append((tables["domains"][b : b + 1, :] == label).astype(f32))
    sums = lax.dot_general(
        jnp.concatenate(left, axis=1), jnp.concatenate(right, axis=1), (((1,), (1,)), ((), ())),
        precision=lax.Precision.HIGHEST, preferred_element_type=f32,
    )
    dbuf[c] = sums

    def last_copy(slot):
        return pltpu.make_async_remote_copy(
            src_ref=dbuf.at[slot], dst_ref=dbuf.at[slot], send_sem=s_send.at[13], recv_sem=s_recv.at[13],
            device_id={"dp_2": other}, device_id_type=MESH,
        )

    last_copy(c).start()
    me = x * 4 + y
    here = jnp.where((owner == me) & (sub < 6), excess, 0.0)
    j = lax.broadcasted_iota(jnp.int32, (128, 128), 0)
    l = lax.broadcasted_iota(jnp.int32, (128, 128), 1)
    sel_ab = (j == l % 16 + jnp.where(l < 64, 0, 16)).astype(f32)
    sel_c = (j == l % 16 + 32).astype(f32)
    spots = jnp.concatenate([jnp.where(sub < 4, here, 0.0), jnp.where(sub >= 4, here, 0.0)], axis=1)
    mine_out = lax.dot_general(
        spots, jnp.concatenate([sel_ab, sel_c], axis=1), (((1,), (1,)), ((), ())),
        precision=lax.Precision.HIGHEST, preferred_element_type=f32,
    )
    mine_row = jnp.sum(mine_out, axis=0, keepdims=True)
    prior = M0[y, 3:4, :]
    weights = prior / jnp.sum(prior, axis=1, keepdims=True)
    last_copy(other).wait_recv()
    both = dbuf[0] + dbuf[1]
    for s in range(STEPS):
        gain = both[s : s + 1, :] / jnp.maximum(both[3 + s : 4 + s, :], 1.0)
        raised = weights * jnp.exp(step_size * gain)
        weights = (1.0 - smoothing) * raised / jnp.sum(raised, axis=1, keepdims=True) + smoothing / DOMAINS
    out[...] = jnp.where(sub == 0, jnp.log(weights), mine_row)

    for i, cp in enumerate(copies):
        gather_copy(i, cp["source"], cp["sign"]).wait_send()
    for (m, dz), s in swaps.items():
        swap_copy(s, m, dz).wait_send()
    for d in (1, 2, 3):
        meta_copy(d - 1, "y", d, True).wait_send()
        meta_copy(2 + d, "x", d, True).wait_send()
    for copy in sent_z + sent_y + sent_x:
        copy.wait_send()
    last_copy(c).wait_send()


def local(ph, rh, pw, rw, targets, domains, keep_mask, prior):
    def line(a):
        return jnp.pad(a.astype(jnp.float32), (0, 128 - a.shape[0]))[None]

    meta = jnp.concatenate(
        [line(targets), line(domains), line(keep_mask), line(prior), jnp.zeros((4, 128), jnp.float32)]
    )
    rows = pw.shape[0]
    copies = gather_plan()
    order = schedule(copies, [(w, group_tokens(*w)) for w in WORK])
    f32, bf16 = jnp.float32, jnp.bfloat16
    dma = pltpu.SemaphoreType.DMA
    anywhere = pl.BlockSpec(memory_space=pl.ANY)

    def body(*refs):
        kernel(copies, order, rows, *refs)

    out = pl.pallas_call(
        body,
        name="doremi",
        out_shape=jax.ShapeDtypeStruct((8, 128), f32),
        in_specs=[anywhere] * 5,
        out_specs=pl.BlockSpec(memory_space=pltpu.VMEM),
        scratch_shapes=[
            pltpu.VMEM((3, 2, 4, 4, 16, 4096), bf16),
            pltpu.VMEM((2, 2, rows, 4096), bf16),
            pltpu.VMEM((2, 2, rows, 128), f32),
            pltpu.VMEM((2, 2, rows, 256), f32),
            pltpu.VMEM((2, 2, rows, 128), f32),
            pltpu.VMEM((2, 2, rows, 256), f32),
            pltpu.VMEM((4, 8, 128), f32),
            pltpu.VMEM((4, 4, 8, 128), f32),
            pltpu.VMEM((3, 8, 128), f32),
            pltpu.VMEM((8, 3, 8, 128), f32),
            pltpu.VMEM((4, 3, 8, 128), f32),
            pltpu.VMEM((4, 3, 8, 128), f32),
            pltpu.VMEM((2, 8, 128), f32),
            dma((7,)), dma((2,)), dma((16,)), dma((16,)),
            dma((len(copies),)), dma((len(copies),)),
            dma((6,)), dma((6,)), dma((14,)), dma((14,)),
        ],
        compiler_params=pltpu.CompilerParams(
            collective_id=0, has_side_effects=True, vmem_limit_bytes=60 * 1024 * 1024
        ),
        cost_estimate=pl.CostEstimate(flops=12_900_000_000, bytes_accessed=34_000_000, transcendentals=2_000_000),
    )(ph, rh, pw, rw, meta)
    return out[1, : targets.shape[0]], out[0]


def solution(mesh):
    split = Mesh(
        mesh.devices.reshape(4, 4, 2, mesh.shape["tensor"]), ("dp_0", "dp_1", "dp_2", "tensor")
    )
    return jax.shard_map(
        local,
        mesh=split,
        in_specs=(
            P(DP, "tensor"),
            P(DP, "tensor"),
            P(DP_TENSOR, None),
            P(DP_TENSOR, None),
            P(DP),
            P(DP),
            P(DP),
            P(),
        ),
        out_specs=(P(DP), P()),
        check_vma=False,
    )
```

time: 223 us -> 94.9 us (0.43)
  the two profiles are of different devices: /device:TPU:2 before, /device:TPU:1 now
where the time goes in v1:
time: 94.9 us; the launch traced here: 94.7 us
  Pallas kernels  88.4 us (93%)
  local copies, waits for them, and re-layouts  3.63 us (4%)
  other arithmetic  1.97 us (2%)
    pallas_call x1, Pallas kernels, local(): pl.pallas_call(body, name='doremi', out_shape=jax.ShapeDtypeStruct((8, 12...  88.4 us
    squeeze x2, local copies, waits for them, and re-layouts, local(): return (out[1, :targets.shape[0]], out[0])  2.37 us
    convert_element_type x3, other arithmetic, line(): return jnp.pad(a.astype(jnp.float32), (0, 128 - a.shape[0]))[None]  1.97 us

profile of v1, /device:TPU:1, one launch (start us, length us, event | category | flops | bytes accessed | tf_op | source)
XLA Modules:
  0.0 94.7 jit_solution(13839399197770404154)
XLA Ops:
  0.6 0.7 convert_element_type.13
  1.3 0.7 convert_element_type.14
  2.0 0.7 convert_element_type.15
  2.6 1.3 %concatenate.3.refs_4_ = f32[8,128]{1,0:T(8,128)} concatenate(f32[1,128]{1,0:T(1,128)S(1)} %pad_bitcast_fusion.2, f32[1,128]{1,0:T(1,128)S(1)} %get-tuple-element.3, f32[1,128]{1,0:T(1,128)S(1)} %get-tuple-element.2, f32[1,128]{1,0:T(1,128)} %bitcast.11, f32[4,128]{1,0:T(4,128)S(1)} %broadcast_in_dim.19), dimensions={0} | concatenate | bytes 8192 | tf_op jit(solution)/shard_map/concatenate | solution.py:484
  3.9 88.4 %doremi.1 = f32[8,128]{1,0:T(8,128)} custom-call(bf16[48,512]{1,0:T(8,128)(2,1)} %refs_0_.1, bf16[48,512]{1,0:T(8,128)(2,1)} %refs_1_.1, bf16[501,4096]{1,0:T(8,128)(2,1)} %refs_2_.1, bf16[501,4096]{1,0:T(8,128)(2,1)} %refs_3_.1, f32[8,128]{1,0:T(8,128)} %concatenate.3.refs_4_), custom_call_target="tpu_custom_call" | custom-call | flops 12899999744 | bytes 34000000 | tf_op jit(solution)/shard_map/doremi/pallas_call | solution.py:497
  92.3 1.2 %slice_bitcast_fusion = f32[128]{0:T(128)} fusion(f32[8,128]{1,0:T(8,128)} %doremi.1), kind=kLoop, calls=%fused_computation | loop fusion | bytes 1024 | tf_op jit(solution)/shard_map/squeeze | solution.py:526
  93.5 1.2 %slice_bitcast_fusion.1 = f32[48]{0:T(128)} fusion(f32[8,128]{1,0:T(8,128)} %doremi.1), kind=kLoop, calls=%fused_computation.1 | loop fusion | bytes 384 | tf_op jit(solution)/shard_map/squeeze | solution.py:526
  (3 shorter events, 0.0 us)

commit v2 on v1

v2 whole, which is shorter than its diff:
```python
import jax
import jax.numpy as jnp
from jax import lax
from jax.experimental import pallas as pl
from jax.experimental.pallas import tpu as pltpu
from jax.sharding import Mesh
from jax.sharding import PartitionSpec as P

DOMAINS = 128
STEPS = 3
DP = ("dp_0", "dp_1", "dp_2")
DP_TENSOR = ("dp_0", "dp_1", "dp_2", "tensor")
AXIS = {"x": "dp_0", "y": "dp_1", "z": "tensor"}
MESH = pl.DeviceIdType.MESH

step_size = 1.0
smoothing = 0.001

KB = 1024
RATE = 46.6e3
HOP = 3.5
BACKLOG = 2.5
LAG = 0.45
FINE = (0, 1, -1)
RING4 = (0, 1, -1, 2)
RING8 = (0, 1, -1, 2, -2, 3, -3, 4)


def ring(add, axis, size, token, need, far, rank, arrival, lag=0.01):
    for k in range(1, far + 1):
        halves = (0, 1) if k == far else (None, None)
        for sign, half in ((1, halves[0]), (-1, halves[1])):
            offset = far if k == far else -sign * k
            add(
                dict(
                    axis=axis,
                    sign=sign,
                    size=size // 2 if k == far else size,
                    source=token(-sign * (k - 1), half),
                    need=need if k == 1 else [token(-sign * (k - 1), None)],
                    given=token(offset, half),
                    rank=rank + lag * (k - 1),
                    arrival=arrival + (offset,),
                )
            )


def gather_plan():
    copies = []
    add = copies.append
    piece = 32 * KB
    for colour, first, last in (("A", "y", "x"), ("B", "x", "y")):
        own = [(colour, "z", 0, None)]
        ring(add, "z", piece, lambda d, h: (colour, "z", d, h), own, 4, 0, (colour, "z"))
        for q, dz in enumerate(RING8):
            have = [(colour, "z", dz, None)]
            ring(add, first, piece, lambda d, h: (colour, "f", dz, d, h), have, 2, 1, (colour, "f", dz))
            rank = 3 + 0.1 * q
            if dz in FINE:
                for df in RING4:
                    need = have if df == 0 else [(colour, "f", dz, df, None)]
                    token = lambda d, h: (colour, "p", dz, df, d, h)
                    ring(add, last, piece, token, need, 2, rank, (colour, "p", dz, df), LAG)
            else:
                need = have + [(colour, "f", dz, d, None) for d in (1, -1, 2)]
                token = lambda d, h: (colour, "l", dz, d, h)
                ring(add, last, 4 * piece, token, need, 2, rank, (colour, "l", dz), LAG)
    piece = 16 * KB
    own = [("C", "o", 0, None)]
    ring(add, "z", 2 * piece, lambda d, h: ("C", "o", d, h), own, 4, 2, ("C", "o"))
    for colour, first, last in (("C0", "x", "y"), ("C1", "y", "x")):
        ring(add, first, piece, lambda d, h: (colour, "f", d, h), own, 2, 0, (colour, "f"))
        need = own + [(colour, "f", d, None) for d in (1, -1, 2)]
        ring(add, last, 4 * piece, lambda d, h: (colour, "l", d, h), need, 2, 0, (colour, "l"))
        for j in (1, -1, 2):
            need = [(colour, "f", j, None)]
            ring(add, "z", piece, lambda d, h: (colour, "y", j, d, h), need, 4, 2, ("C", "y", j))
        for j in (1, -1, 2):
            need = [(colour, "l", j, None)]
            ring(add, "z", 4 * piece, lambda d, h: (colour, "z", j, d, h), need, 4, 2, ("C", "z", j))
    return copies


OWN = {("A", "z", 0, None), ("B", "z", 0, None), ("C", "o", 0, None)}


def tokens_of(group, dzs):
    out = []
    for dz in dzs:
        if group == "C":
            if dz:
                out.append(("C", "o", dz, None))
            for colour in ("C0", "C1"):
                for j in (1, -1, 2):
                    if dz:
                        out += [(colour, "y", j, dz, None), (colour, "z", j, dz, None)]
                    else:
                        out += [(colour, "f", j, None), (colour, "l", j, None)]
            continue
        for colour in ("A", "B"):
            if group == 0:
                out += [(colour, "z", dz, None)] + [(colour, "f", dz, d, None) for d in (1, -1, 2)]
                continue
            for d in (1, -1) if group == 1 else (2,):
                if dz in FINE:
                    out += [(colour, "p", dz, df, d, None) for df in RING4]
                else:
                    out.append((colour, "l", dz, d, None))
    return out


WORK = [
    (0, (0,)), (0, (1, -1)), (0, (2, -2)), (0, (3, -3, 4)),
    (1, (0,)), (1, (1, -1)), (1, (2, -2)), (1, (3, -3)), (1, (4,)),
    (2, (0,)), (2, (1, -1)), (2, (2, -2)), (2, (3, -3)), (2, (4,)),
    ("C", (0,)), ("C", (1, -1)), ("C", (2, -2)), ("C", (3, -3)), ("C", (4,)),
]
STATS_TIME = {0: 0.34, 1: 0.74, 2: 0.34, "C": 0.74}


def schedule(copies, works):
    arrival_of = {c["given"]: c["arrival"] for c in copies}
    members = {}
    for i, c in enumerate(copies):
        members.setdefault(c["arrival"], []).append(i)

    def arrivals(tokens):
        found = set()
        for t in tokens:
            if t not in OWN:
                found |= {arrival_of[p] for p in (t, t[:-1] + (0,), t[:-1] + (1,)) if p in arrival_of}
        return found

    deps = [arrivals(c["need"]) for c in copies]
    needs = [arrivals(tokens_of(*w)) for w in works]
    links = {}
    for i, c in enumerate(copies):
        links.setdefault((c["axis"], c["sign"]), []).append(i)
    got, free, landed = set(), dict.fromkeys(links, 0.0), {}
    unsent, undone = set(range(len(copies))), set(range(len(works)))
    left = {g: sum(1 for w in works if w[0] == g) for g in STATS_TIME}
    now, order = 0.0, []
    while unsent or undone or len(got) < len(members):
        coming = {
            a: max(landed[i] for i in m)
            for a, m in members.items()
            if a not in got and all(i in landed for i in m)
        }
        here = sorted((when, str(a), a) for a, when in coming.items() if when <= now + 1e-9)
        if here:
            for _, _, a in here:
                got.add(a)
                order.append(("recv", a))
                now += 0.02
            continue
        sent = False
        for link, all_of in links.items():
            while free[link] - now < BACKLOG:
                ready = [i for i in all_of if i in unsent and deps[i] <= got]
                if not ready:
                    break
                i = min(ready, key=lambda i: (copies[i]["rank"], i))
                free[link] = max(now, free[link]) + copies[i]["size"] / RATE
                landed[i] = free[link] + HOP
                unsent.discard(i)
                order.append(("send", i))
                now += 0.012
                sent = True
        if sent:
            continue
        ready = [i for i in undone if needs[i] <= got]
        if ready:
            i = min(ready)
            undone.discard(i)
            order.append(("compute", i))
            now += 0.35 + 0.54 * len(works[i][1])
            left[works[i][0]] -= 1
            if not left[works[i][0]]:
                now += STATS_TIME[works[i][0]]
            continue
        times = list(coming.values())
        for link, all_of in links.items():
            if any(i in unsent and deps[i] <= got for i in all_of):
                times.append(free[link] - BACKLOG + 1e-6)
        now = max(now, min(times))
    return order


SEND_CLASS = {
    ("A", "z"): 0, ("A", "f"): 1, ("A", "p"): 2, ("A", "l"): 2,
    ("B", "z"): 3, ("B", "f"): 4, ("B", "p"): 5, ("B", "l"): 5,
    ("C", "o"): 6, ("C0", "y"): 6, ("C1", "y"): 6, ("C0", "z"): 6, ("C1", "z"): 6,
    ("C0", "f"): 7, ("C1", "f"): 7, ("C0", "l"): 8, ("C1", "l"): 8,
}


def kernel(
    copies, order, rows, tokens,
    ph, rh, pw, rw, tg, dm, kp, pr, out_excess, out_weights,
    G, W, acc0, acc1, acc2, accC, tgv, dmv, kpv, prv, M0, M1, st, zbuf, ybuf, xbuf, dbuf,
    own_sem, small_sem, head_sem, swap_send, swap_recv, g_send, g_recv, m_send, m_recv, s_send, s_recv,
):
    x, y, c, z = (lax.axis_index(a) for a in ("dp_0", "dp_1", "dp_2", "tensor"))
    other = 1 - c
    pos = {"x": (x, 4), "y": (y, 4), "z": (z, 8)}

    def at(axis, d):
        p, n = pos[axis]
        return lax.rem(p + (d % n), n) if d % n else p

    def peer(axis, d):
        return {AXIS[axis]: at(axis, d)}

    def cols(dz, half=None):
        begin = at("z", dz) * 512
        if half is None:
            return pl.ds(pl.multiple_of(begin, 512), 512)
        return pl.ds(pl.multiple_of(begin + 256 * half, 256), 256)

    def view(token):
        colour, phase, half = token[0], token[1], token[-1]
        ms = slice(0, 2) if half is None else half
        if colour in ("A", "B"):
            k = 0 if colour == "A" else 1
            last, first = ("x", "y") if colour == "A" else ("y", "x")
            dz = token[2]
            if phase == "z":
                return G.at[k, ms, at(last, 0), at(first, 0), :, cols(dz)]
            if phase == "f":
                return G.at[k, ms, at(last, 0), at(first, token[3]), :, cols(dz)]
            if phase == "p":
                return G.at[k, ms, at(last, token[4]), at(first, token[3]), :, cols(dz)]
            return G.at[k, ms, at(last, token[3]), :, :, cols(dz)]
        d = token[2]
        if colour == "C":
            return G.at[2, ms, x, y, :, cols(d)]
        if phase in ("f", "y"):
            cs = cols(0 if phase == "f" else token[3], half)
            if colour == "C0":
                return G.at[2, 0, at("x", d), y, :, cs]
            return G.at[2, 1, x, at("y", d), :, cs]
        cs = cols(0 if phase == "l" else token[3], half)
        if colour == "C0":
            return G.at[2, 0, :, at("y", d), :, cs]
        return G.at[2, 1, at("x", d), :, :, cs]

    arrival_at = {}
    for cp in copies:
        arrival_at.setdefault(cp["arrival"], [len(arrival_at), 0])[1] += cp["size"]
    amounts = {
        16 * KB: G.at[0, 0, 0, 0, :, pl.ds(0, 512)],
        32 * KB: G.at[0, :, 0, 0, :, pl.ds(0, 512)],
        64 * KB: G.at[0, 0, 0, :, :, pl.ds(0, 512)],
        128 * KB: G.at[0, :, 0, :, :, pl.ds(0, 512)],
    }

    def wait(ref, sem):
        pltpu.make_async_copy(ref, ref, sem).wait()

    def send(i):
        cp = copies[i]
        ref = view(cp["source"])
        pltpu.make_async_remote_copy(
            src_ref=ref, dst_ref=ref,
            send_sem=g_send.at[SEND_CLASS[cp["source"][:2]]], recv_sem=g_recv.at[arrival_at[cp["arrival"]][0]],
            device_id=peer(cp["axis"], cp["sign"]), device_id_type=MESH,
        ).start()

    def receive(arrival):
        index, size = arrival_at[arrival]
        wait(amounts[size], g_recv.at[index])

    for k, (src, dst) in enumerate(((tg, tgv), (dm, dmv), (kp, kpv), (pr, prv))):
        pltpu.make_async_copy(src, dst, small_sem.at[k]).start()
    for m, src in enumerate((ph, rh)):
        for k in range(3):
            dst = G.at[k, m, y, x, :, cols(0)] if k == 1 else G.at[k, m, x, y, :, cols(0)]
            pltpu.make_async_copy(src.at[pl.ds(16 * k, 16), :], dst, own_sem).start()
    heads = (pw, rw)
    for m in (0, 1):
        pltpu.make_async_copy(heads[m], W.at[m, 0], head_sem).start()

    barrier = pltpu.get_barrier_semaphore()
    peers = [peer("z", d) for d in range(1, 8)] + [peer(a, d) for a in "xy" for d in (1, 2, 3)]
    peers.append({"dp_2": other})
    for target in peers:
        pl.semaphore_signal(barrier, inc=1, device_id=target, device_id_type=MESH)
    st[...] = jnp.zeros_like(st)
    M0[y] = jnp.zeros((8, 128), jnp.float32)
    for k, (src, dst) in enumerate(((tg, tgv), (dm, dmv), (kp, kpv), (pr, prv))):
        pltpu.make_async_copy(src, dst, small_sem.at[k]).wait()
    for k, ref in enumerate((tgv, dmv, kpv)):
        M0[y, k : k + 1, 0:tokens] = ref[...].astype(jnp.float32)
    with jax.named_scope("entry_barrier"):
        pl.semaphore_wait(barrier, len(peers))
    with jax.named_scope("own_blocks"):
        wait(G.at[:, :, 0, 0, :, pl.ds(0, 512)], own_sem)

    def meta_send(axis, d):
        src, dst, k = (M0.at[y], M0.at[y], 0) if axis == "y" else (M0, M1.at[x], 1)
        pltpu.make_async_remote_copy(
            src_ref=src, dst_ref=dst, send_sem=m_send.at[k], recv_sem=m_recv.at[k],
            device_id=peer(axis, d), device_id_type=MESH,
        ).start()

    def swap(m, dz, q):
        pltpu.make_async_remote_copy(
            src_ref=heads[m].at[:, cols(dz)], dst_ref=W.at[m, 1, :, cols(dz)],
            send_sem=swap_send, recv_sem=swap_recv.at[q],
            device_id={"dp_2": other}, device_id_type=MESH,
        ).start()

    f32 = jnp.float32
    lane = lax.broadcasted_iota(jnp.int32, (8, 128), 1)
    sub = lax.broadcasted_iota(jnp.int32, (8, 128), 0)
    accs = {0: acc0, 1: acc1, 2: acc2, "C": accC}

    def block(group, m, dz):
        cs = cols(dz)
        if group == "C":
            return G[2, m, :, :, :, cs].reshape(256, 512)
        pieces = []
        for d in {0: (0,), 1: (-1, 1), 2: (2,)}[group]:
            pieces.append(G[0, m, at("x", d), :, :, cs].reshape(64, 512))
            pieces.append(G[1, m, at("y", d), :, :, cs].reshape(64, 512))
        return jnp.concatenate(pieces, axis=0)

    done_heads = set()

    def compute(i):
        group, dzs = WORK[i]
        if not done_heads:
            wait(W.at[:, 0], head_sem)
        for dz in dzs:
            if dz not in done_heads:
                wait(W.at[:, 1, :, cols(dz)], swap_recv.at[RING8.index(dz)])
                done_heads.add(dz)
        acc = accs[group]
        first = 0 in dzs

        def body(m, carry):
            rhs = [block(group, m, dz) for dz in dzs]
            for h in (0, 1):
                total = None
                for dz, r in zip(dzs, rhs):
                    part = lax.dot_general(
                        W[m, h, :, cols(dz)], r, (((1,), (1,)), ((), ())), preferred_element_type=f32
                    )
                    total = part if total is None else total + part
                acc[m, h] = total if first else acc[m, h] + total
            return carry

        lax.fori_loop(0, 2, body, 0)

    dev = ((x * 4 + y) * 2 + c) * 8 + z
    dev_other = ((x * 4 + y) * 2 + other) * 8 + z
    offsets = (dev * rows, dev_other * rows)

    def spread(quantity):
        j = lax.broadcasted_iota(jnp.int32, (128, 128), 0)
        l = lax.broadcasted_iota(jnp.int32, (128, 128), 1)
        low = l % 16
        sel_ab = (j == low + jnp.where(l < 64, 0, 16)).astype(f32)
        sel_c = (j == low + 32).astype(f32)
        ab = jnp.dot(quantity, sel_ab, precision=lax.Precision.HIGHEST, preferred_element_type=f32)
        cc = jnp.dot(quantity, sel_c, precision=lax.Precision.HIGHEST, preferred_element_type=f32)
        d = lax.broadcasted_iota(jnp.int32, (16, 128), 0)
        l = lax.broadcasted_iota(jnp.int32, (16, 128), 1)
        q = (l // 16) % 4
        result = jnp.zeros((8, 128), f32)
        for a in range(4):
            owner = jnp.where(l < 64, a * 4 + q, q * 4 + a)
            row = jnp.sum(jnp.where(d == owner, ab, 0.0), axis=0, keepdims=True)
            result = jnp.where(sub == a, row, result)
        for a in range(2):
            owner = (2 * a + l // 64) * 4 + q
            row = jnp.sum(jnp.where(d == owner, cc, 0.0), axis=0, keepdims=True)
            result = jnp.where(sub == 4 + a, row, result)
        return result

    def stats(group, wanted):
        acc = accs[group]
        width = acc.shape[-1]
        if group == "C":
            places = [sub == 4, sub == 5]
        else:
            places = [
                sub == jnp.where(lane < 64, at("x", d), at("y", d))
                for d in {0: (0,), 1: (-1, 1), 2: (2,)}[group]
            ]
        want = [jnp.sum(jnp.where(p, wanted, 0.0), axis=0, keepdims=True) for p in places]
        want = jnp.concatenate(want, axis=1).astype(jnp.int32) if len(want) > 1 else want[0].astype(jnp.int32)
        vocab = lax.broadcasted_iota(jnp.int32, (rows, width), 0)
        lses, hits = [], []
        for m in (0, 1):
            peak = jnp.maximum(
                jnp.max(acc[m, 0], axis=0, keepdims=True), jnp.max(acc[m, 1], axis=0, keepdims=True)
            )
            total = jnp.zeros((1, width), f32)
            hit = jnp.zeros((1, width), f32)
            for h in (0, 1):
                logits = acc[m, h]
                total += jnp.sum(jnp.exp(logits - peak), axis=0, keepdims=True)
                match = vocab == want - offsets[h]
                hit += jnp.sum(jnp.where(match, logits, 0.0), axis=0, keepdims=True)
            lses.append(peak + jnp.log(total))
            hits.append(hit)
        for k, row in enumerate((lses[0], lses[1], hits[0] - hits[1])):
            value = st[k]
            for b, place in enumerate(places):
                value = jnp.where(place, row[:, 128 * b : 128 * (b + 1)], value)
            st[k] = value

    tables = {}
    pending = {g: sum(1 for w in WORK if w[0] == g) for g in accs}
    steps = 0
    for kind, i in order:
        if kind == "send":
            send(i)
        elif kind == "recv":
            if not steps:
                for d in (1, 2, 3):
                    meta_send("y", d)
                for q, dz in enumerate(RING8):
                    for m in (0, 1):
                        swap(m, dz, q)
            steps += 1
            with jax.named_scope("recv"):
                receive(i)
        else:
            if not done_heads:
                wait(M0.at[pl.ds(0, 3)], m_recv.at[0])
                M1[x] = M0[...]
                for d in (1, 2, 3):
                    meta_send("x", d)
            with jax.named_scope(f"compute_{i}"):
                compute(i)
            group = WORK[i][0]
            pending[group] -= 1
            if not pending[group]:
                if not tables:
                    wait(M1.at[pl.ds(0, 3)], m_recv.at[1])
                    for k, name in enumerate(("targets", "domains", "keep")):
                        tables[name] = spread(M1[:, :, k, :].reshape(16, 128))
                with jax.named_scope(f"stats_{group}"):
                    stats(group, tables["targets"])

    def exchange(buf, axis, stage):
        n, mine = pos[axis][1], pos[axis][0]
        for d in range(1, n):
            pltpu.make_async_remote_copy(
                src_ref=buf.at[mine], dst_ref=buf.at[mine],
                send_sem=s_send.at[stage], recv_sem=s_recv.at[stage],
                device_id=peer(axis, d), device_id_type=MESH,
            ).start()
        wait(buf.at[pl.ds(0, n - 1)], s_recv.at[stage])
        parts = [[buf[s, k] for k in range(3)] for s in range(n)]
        combined = []
        for k in (0, 1):
            peak = parts[0][k]
            for s in range(1, n):
                peak = jnp.maximum(peak, parts[s][k])
            total = jnp.exp(parts[0][k] - peak)
            for s in range(1, n):
                total = total + jnp.exp(parts[s][k] - peak)
            combined.append(peak + jnp.log(total))
        hit = parts[0][2]
        for s in range(1, n):
            hit = hit + parts[s][2]
        combined.append(hit)
        return combined

    zbuf[z] = st[...]
    with jax.named_scope("exchange_z"):
        result = exchange(zbuf, "z", 0)
    for k in range(3):
        ybuf[y, k] = result[k]
    with jax.named_scope("exchange_y"):
        result = exchange(ybuf, "y", 1)
    for k in range(3):
        xbuf[x, k] = result[k]
    with jax.named_scope("exchange_x"):
        lse0, lse1, hit = exchange(xbuf, "x", 2)

    keep = tables["keep"]
    gap = (lse0 - lse1) - hit
    excess = gap * keep
    clipped = jnp.maximum(gap, 0.0) * keep
    q = (lane // 16) % 4
    low = lane % 16
    owner = jnp.where(sub < 4, jnp.where(lane < 64, sub * 4 + q, q * 4 + sub), (2 * (sub - 4) + lane // 64) * 4 + q)
    colour = jnp.where(sub < 4, jnp.where(lane < 64, 0, 1), 2)
    token = (owner * 2 + c) * 48 + 16 * colour + low
    batch = token // 512
    label = lax.broadcasted_iota(jnp.int32, (128, 128), 0).astype(f32)
    left, right = [], []
    for b in range(6):
        bb = batch[b : b + 1, :]
        top = jnp.where(bb == sub, clipped[b : b + 1, :], 0.0)
        low_rows = jnp.where(bb == sub - 3, keep[b : b + 1, :], 0.0)
        left.append(jnp.where(sub < 3, top, low_rows))
        right.append((tables["domains"][b : b + 1, :] == label).astype(f32))
    sums = lax.dot_general(
        jnp.concatenate(left, axis=1), jnp.concatenate(right, axis=1), (((1,), (1,)), ((), ())),
        precision=lax.Precision.HIGHEST, preferred_element_type=f32,
    )
    dbuf[c] = sums

    def last_copy(slot):
        return pltpu.make_async_remote_copy(
            src_ref=dbuf.at[slot], dst_ref=dbuf.at[slot], send_sem=s_send.at[3], recv_sem=s_recv.at[3],
            device_id={"dp_2": other}, device_id_type=MESH,
        )

    last_copy(c).start()
    me = x * 4 + y
    here = jnp.where((owner == me) & (sub < 6), excess, 0.0)
    j = lax.broadcasted_iota(jnp.int32, (128, 128), 0)
    l = lax.broadcasted_iota(jnp.int32, (128, 128), 1)
    sel_ab = (j == l % 16 + jnp.where(l < 64, 0, 16)).astype(f32)
    sel_c = (j == l % 16 + 32).astype(f32)
    spots = jnp.concatenate([jnp.where(sub < 4, here, 0.0), jnp.where(sub >= 4, here, 0.0)], axis=1)
    mine_out = lax.dot_general(
        spots, jnp.concatenate([sel_ab, sel_c], axis=1), (((1,), (1,)), ((), ())),
        precision=lax.Precision.HIGHEST, preferred_element_type=f32,
    )
    mine_row = jnp.sum(mine_out, axis=0, keepdims=True)
    prior = prv[...]
    weights = prior / jnp.sum(prior, axis=1, keepdims=True)
    with jax.named_scope("partner_sums"):
        last_copy(other).wait_recv()
    both = dbuf[0] + dbuf[1]
    for s in range(STEPS):
        gain = both[s : s + 1, :] / jnp.maximum(both[3 + s : 4 + s, :], 1.0)
        raised = weights * jnp.exp(step_size * gain)
        weights = (1.0 - smoothing) * raised / jnp.sum(raised, axis=1, keepdims=True) + smoothing / DOMAINS
    out_weights[...] = jnp.log(weights)
    out_excess[...] = mine_row[:, 0:tokens]

    with jax.named_scope("sends_done"):
        for k in range(2):
            wait(G.at[k, :, 0, 0, :, pl.ds(0, 7 * 512)], g_send.at[3 * k])
            wait(G.at[k, :, 0, pl.ds(0, 3)], g_send.at[3 * k + 1])
            wait(G.at[k, :, pl.ds(0, 3)], g_send.at[3 * k + 2])
        wait(G.at[2, :, :, :, :, pl.ds(0, 7 * 512)], g_send.at[6])
        wait(G.at[2, :, pl.ds(0, 3), 0, :, pl.ds(0, 512)], g_send.at[7])
        wait(G.at[2, :, pl.ds(0, 3), :, :, pl.ds(0, 512)], g_send.at[8])
        wait(W.at[:, 1], swap_send)
        wait(M0.at[pl.ds(0, 3)], m_send.at[0])
        wait(M1.at[pl.ds(0, 3)], m_send.at[1])
        wait(zbuf.at[pl.ds(0, 7)], s_send.at[0])
        wait(ybuf.at[pl.ds(0, 3)], s_send.at[1])
        wait(xbuf.at[pl.ds(0, 3)], s_send.at[2])
        last_copy(c).wait_send()


def local(ph, rh, pw, rw, targets, domains, keep_mask, prior):
    rows, tokens = pw.shape[0], targets.shape[0]
    copies = gather_plan()
    order = schedule(copies, WORK)
    arrivals = len({c["arrival"] for c in copies})
    f32, bf16 = jnp.float32, jnp.bfloat16
    dma = pltpu.SemaphoreType.DMA
    anywhere = pl.BlockSpec(memory_space=pl.ANY)

    def body(*refs):
        kernel(copies, order, rows, tokens, *refs)

    out = pl.pallas_call(
        body,
        name="doremi",
        out_shape=[jax.ShapeDtypeStruct((1, tokens), f32), jax.ShapeDtypeStruct((1, 128), f32)],
        in_specs=[anywhere] * 8,
        out_specs=[pl.BlockSpec(memory_space=pltpu.VMEM)] * 2,
        scratch_shapes=[
            pltpu.VMEM((3, 2, 4, 4, 16, 4096), bf16),
            pltpu.VMEM((2, 2, rows, 4096), bf16),
            pltpu.VMEM((2, 2, rows, 128), f32),
            pltpu.VMEM((2, 2, rows, 256), f32),
            pltpu.VMEM((2, 2, rows, 128), f32),
            pltpu.VMEM((2, 2, rows, 256), f32),
            pltpu.VMEM((1, tokens), jnp.int32),
            pltpu.VMEM((1, tokens), jnp.int32),
            pltpu.VMEM((1, tokens), jnp.int32),
            pltpu.VMEM((1, 128), f32),
            pltpu.VMEM((4, 8, 128), f32),
            pltpu.VMEM((4, 4, 8, 128), f32),
            pltpu.VMEM((3, 8, 128), f32),
            pltpu.VMEM((8, 3, 8, 128), f32),
            pltpu.VMEM((4, 3, 8, 128), f32),
            pltpu.VMEM((4, 3, 8, 128), f32),
            pltpu.VMEM((2, 8, 128), f32),
            dma, dma((4,)), dma, dma, dma((8,)),
            dma((9,)), dma((arrivals,)),
            dma((2,)), dma((2,)), dma((4,)), dma((4,)),
        ],
        compiler_params=pltpu.CompilerParams(
            collective_id=0, has_side_effects=True, vmem_limit_bytes=60 * 1024 * 1024
        ),
        cost_estimate=pl.CostEstimate(flops=12_900_000_000, bytes_accessed=34_000_000, transcendentals=2_000_000),
    )(ph, rh, pw, rw, targets[None], domains[None], keep_mask[None], prior[None])
    return out[0][0], out[1][0]


def solution(mesh):
    split = Mesh(
        mesh.devices.reshape(4, 4, 2, mesh.shape["tensor"]), ("dp_0", "dp_1", "dp_2", "tensor")
    )
    return jax.shard_map(
        local,
        mesh=split,
        in_specs=(
            P(DP, "tensor"),
            P(DP, "tensor"),
            P(DP_TENSOR, None),
            P(DP_TENSOR, None),
            P(DP),
            P(DP),
            P(DP),
            P(),
        ),
        out_specs=(P(DP), P()),
        check_vma=False,
    )
```

time: 94.9 us -> 83.1 us (0.88)
  Pallas kernels: 88.4 us -> 80.1 us
  other arithmetic: 1.97 us -> 0 us
  local copies, waits for them, and re-layouts: 3.63 us -> 2.25 us
    pallas_call x1, Pallas kernels: 88.4 us -> 80.1 us  [local(): pl.pallas_call(body, name='doremi', out_shape=[jax.ShapeDtypeStruct((1, t...]
    squeeze x2 -> x0, local copies, waits for them, and re-layouts: 2.37 us -> none  [local(): return (out[1, :targets.shape[0]], out[0])]
    unnamed x0 -> x2, local copies, waits for them, and re-layouts: none -> 2.25 us
    convert_element_type x3 -> x0, other arithmetic: 1.97 us -> none  [line(): return jnp.pad(a.astype(jnp.float32), (0, 128 - a.shape[0]))[None]]
    concatenate x1 -> x0, local copies, waits for them, and re-layouts: 1.25 us -> none  [local(): jnp.concatenate([line(targets), line(domains), line(keep_mask), line(prio...]
where the time goes in v2:
time: 83.1 us; the launch traced here: 83 us
  Pallas kernels  80.1 us (96%)
  local copies, waits for them, and re-layouts  2.25 us (3%)
    pallas_call x1, Pallas kernels, local(): pl.pallas_call(body, name='doremi', out_shape=[jax.ShapeDtypeStruct((1, t...  80.1 us
    unnamed x2, local copies, waits for them, and re-layouts  2.25 us

profile of v2, /device:TPU:1, one launch (start us, length us, event | category | flops | bytes accessed | tf_op | source)
XLA Modules:
  0.0 83.0 jit_solution(17060459869347560084)
XLA Ops:
  0.6 80.1 %doremi.1 = (f32[1,48]{1,0:T(1,128)}, f32[1,128]{1,0:T(1,128)}) custom-call(bf16[48,512]{1,0:T(8,128)(2,1)} %refs_0_.1, bf16[48,512]{1,0:T(8,128)(2,1)} %refs_1_.1, bf16[501,4096]{1,0:T(8,128)(2,1)} %refs_2_.1, bf16[501,4096]{1,0:T(8,128)(2,1)} %refs_3_.1, s32[1,48]{1,0:T(1,128)} %bitcast.6, s32[1,48]{1,0:T(1,128)} %bitcast.7, s32[1,48]{1,0:T(1,128)} %bitcast.8, ...), custom_call_target="tpu_custom_call" | custom-call | flops 12899999744 | bytes 34000000 | tf_op jit(solution)/shard_map/doremi/pallas_call | solution.py:569
  80.7 1.1 %copy.12 = f32[48]{0:T(128)} copy(f32[48]{0:T(128)} %bitcast.11) | data formatting | bytes 384
  81.8 1.1 %copy.13 = f32[128]{0:T(128)} copy(f32[128]{0:T(128)} %bitcast.10) | data formatting | bytes 1024

commit v3 on v2

--- a/solution.py
+++ b/solution.py
@@ -19,8 +19,8 @@
 KB = 1024
 RATE = 46.6e3
 HOP = 3.5
-BACKLOG = 2.5
-LAG = 0.45
+BACKLOG = 1.5
+LAG = 0.6
 FINE = (0, 1, -1)
 RING4 = (0, 1, -1, 2)
 RING8 = (0, 1, -1, 2, -2, 3, -3, 4)
@@ -51,27 +51,27 @@
     piece = 32 * KB
     for colour, first, last in (("A", "y", "x"), ("B", "x", "y")):
         own = [(colour, "z", 0, None)]
-        ring(add, "z", piece, lambda d, h: (colour, "z", d, h), own, 4, 0, (colour, "z"))
+        ring(add, "z", piece, lambda d, h: (colour, "z", d, h), own, 4, 0, ("AB", "z"))
         for q, dz in enumerate(RING8):
             have = [(colour, "z", dz, None)]
-            ring(add, first, piece, lambda d, h: (colour, "f", dz, d, h), have, 2, 1, (colour, "f", dz))
+            ring(add, first, piece, lambda d, h: (colour, "f", dz, d, h), have, 2, 1, ("AB", "f", dz))
             rank = 3 + 0.1 * q
             if dz in FINE:
                 for df in RING4:
                     need = have if df == 0 else [(colour, "f", dz, df, None)]
                     token = lambda d, h: (colour, "p", dz, df, d, h)
-                    ring(add, last, piece, token, need, 2, rank, (colour, "p", dz, df), LAG)
+                    ring(add, last, piece, token, need, 2, rank, ("AB", "p", dz, abs(df)), LAG)
             else:
                 need = have + [(colour, "f", dz, d, None) for d in (1, -1, 2)]
                 token = lambda d, h: (colour, "l", dz, d, h)
-                ring(add, last, 4 * piece, token, need, 2, rank, (colour, "l", dz), LAG)
+                ring(add, last, 4 * piece, token, need, 2, rank, ("AB", "l", dz), LAG)
     piece = 16 * KB
     own = [("C", "o", 0, None)]
     ring(add, "z", 2 * piece, lambda d, h: ("C", "o", d, h), own, 4, 2, ("C", "o"))
     for colour, first, last in (("C0", "x", "y"), ("C1", "y", "x")):
-        ring(add, first, piece, lambda d, h: (colour, "f", d, h), own, 2, 0, (colour, "f"))
+        ring(add, first, piece, lambda d, h: (colour, "f", d, h), own, 2, 0, ("C", "f"))
         need = own + [(colour, "f", d, None) for d in (1, -1, 2)]
-        ring(add, last, 4 * piece, lambda d, h: (colour, "l", d, h), need, 2, 0, (colour, "l"))
+        ring(add, last, 4 * piece, lambda d, h: (colour, "l", d, h), need, 2, 0, ("C", "l"))
         for j in (1, -1, 2):
             need = [(colour, "f", j, None)]
             ring(add, "z", piece, lambda d, h: (colour, "y", j, d, h), need, 4, 2, ("C", "y", j))
@@ -173,7 +173,7 @@
             i = min(ready)
             undone.discard(i)
             order.append(("compute", i))
-            now += 0.35 + 0.54 * len(works[i][1])
+            now += 0.25 + 0.54 * len(works[i][1])
             left[works[i][0]] -= 1
             if not left[works[i][0]]:
                 now += STATS_TIME[works[i][0]]
@@ -248,10 +248,10 @@
     for cp in copies:
         arrival_at.setdefault(cp["arrival"], [len(arrival_at), 0])[1] += cp["size"]
     amounts = {
-        16 * KB: G.at[0, 0, 0, 0, :, pl.ds(0, 512)],
         32 * KB: G.at[0, :, 0, 0, :, pl.ds(0, 512)],
         64 * KB: G.at[0, 0, 0, :, :, pl.ds(0, 512)],
         128 * KB: G.at[0, :, 0, :, :, pl.ds(0, 512)],
+        256 * KB: G.at[0:2, :, 0, :, :, pl.ds(0, 512)],
     }
 
     def wait(ref, sem):
@@ -270,12 +270,13 @@
         index, size = arrival_at[arrival]
         wait(amounts[size], g_recv.at[index])
 
-    for k, (src, dst) in enumerate(((tg, tgv), (dm, dmv), (kp, kpv), (pr, prv))):
-        pltpu.make_async_copy(src, dst, small_sem.at[k]).start()
     for m, src in enumerate((ph, rh)):
         for k in range(3):
             dst = G.at[k, m, y, x, :, cols(0)] if k == 1 else G.at[k, m, x, y, :, cols(0)]
             pltpu.make_async_copy(src.at[pl.ds(16 * k, 16), :], dst, own_sem).start()
+    small = ((tg, tgv), (dm, dmv), (kp, kpv), (pr, prv))
+    for k, (src, dst) in enumerate(small):
+        pltpu.make_async_copy(src, dst, small_sem.at[k]).start()
     heads = (pw, rw)
     for m in (0, 1):
         pltpu.make_async_copy(heads[m], W.at[m, 0], head_sem).start()
@@ -287,10 +288,6 @@
         pl.semaphore_signal(barrier, inc=1, device_id=target, device_id_type=MESH)
     st[...] = jnp.zeros_like(st)
     M0[y] = jnp.zeros((8, 128), jnp.float32)
-    for k, (src, dst) in enumerate(((tg, tgv), (dm, dmv), (kp, kpv), (pr, prv))):
-        pltpu.make_async_copy(src, dst, small_sem.at[k]).wait()
-    for k, ref in enumerate((tgv, dmv, kpv)):
-        M0[y, k : k + 1, 0:tokens] = ref[...].astype(jnp.float32)
     with jax.named_scope("entry_barrier"):
         pl.semaphore_wait(barrier, len(peers))
     with jax.named_scope("own_blocks"):
@@ -338,7 +335,7 @@
         acc = accs[group]
         first = 0 in dzs
 
-        def body(m, carry):
+        for m in (0, 1):
             rhs = [block(group, m, dz) for dz in dzs]
             for h in (0, 1):
                 total = None
@@ -348,9 +345,6 @@
                     )
                     total = part if total is None else total + part
                 acc[m, h] = total if first else acc[m, h] + total
-            return carry
-
-        lax.fori_loop(0, 2, body, 0)
 
     dev = ((x * 4 + y) * 2 + c) * 8 + z
     dev_other = ((x * 4 + y) * 2 + other) * 8 + z
@@ -419,11 +413,16 @@
             send(i)
         elif kind == "recv":
             if not steps:
-                for d in (1, 2, 3):
-                    meta_send("y", d)
+                with jax.named_scope("small_inputs"):
+                    for k, (src, dst) in enumerate(small):
+                        pltpu.make_async_copy(src, dst, small_sem.at[k]).wait()
+                for k, ref in enumerate((tgv, dmv, kpv)):
+                    M0[y, k : k + 1, 0:tokens] = ref[...].astype(f32)
                 for q, dz in enumerate(RING8):
                     for m in (0, 1):
                         swap(m, dz, q)
+                for d in (1, 2, 3):
+                    meta_send("y", d)
             steps += 1
             with jax.named_scope("recv"):
                 receive(i)
@@ -447,7 +446,7 @@
 
     def exchange(buf, axis, stage):
         n, mine = pos[axis][1], pos[axis][0]
-        for d in range(1, n):
+        for d in (4, 3, 5, 2, 6, 1, 7) if n == 8 else (2, 1, 3):
             pltpu.make_async_remote_copy(
                 src_ref=buf.at[mine], dst_ref=buf.at[mine],
                 send_sem=s_send.at[stage], recv_sem=s_recv.at[stage],
@@ -561,7 +560,8 @@
     arrivals = len({c["arrival"] for c in copies})
     f32, bf16 = jnp.float32, jnp.bfloat16
     dma = pltpu.SemaphoreType.DMA
-    anywhere = pl.BlockSpec(memory_space=pl.ANY)
+    anywhere = pl.BlockSpec(memory_space=pltpu.HBM)
+    inside = pl.BlockSpec(memory_space=pltpu.VMEM)
 
     def body(*refs):
         kernel(copies, order, rows, tokens, *refs)
@@ -571,7 +571,7 @@
         name="doremi",
         out_shape=[jax.ShapeDtypeStruct((1, tokens), f32), jax.ShapeDtypeStruct((1, 128), f32)],
         in_specs=[anywhere] * 8,
-        out_specs=[pl.BlockSpec(memory_space=pltpu.VMEM)] * 2,
+        out_specs=[inside] * 2,
         scratch_shapes=[
             pltpu.VMEM((3, 2, 4, 4, 16, 4096), bf16),
             pltpu.VMEM((2, 2, rows, 4096), bf16),
@@ -595,10 +595,13 @@
             dma((2,)), dma((2,)), dma((4,)), dma((4,)),
         ],
         compiler_params=pltpu.CompilerParams(
-            collective_id=0, has_side_effects=True, vmem_limit_bytes=60 * 1024 * 1024
+            collective_id=0, has_side_effects=True, vmem_limit_bytes=53 * 1024 * 1024
         ),
         cost_estimate=pl.CostEstimate(flops=12_900_000_000, bytes_accessed=34_000_000, transcendentals=2_000_000),
-    )(ph, rh, pw, rw, targets[None], domains[None], keep_mask[None], prior[None])
+    )(*(
+        pltpu.with_memory_space_constraint(a, pltpu.HBM)
+        for a in (ph, rh, pw, rw, targets[None], domains[None], keep_mask[None], prior[None])
+    ))
     return out[0][0], out[1][0]
 
 

time: 83.1 us -> 78.7 us (0.947)
  Pallas kernels: 80.1 us -> 77 us
  local copies, waits for them, and re-layouts: 2.25 us -> 1.02 us
    pallas_call x1, Pallas kernels: 80.1 us -> 77 us  [local(): pl.pallas_call(body, name='doremi', out_shape=[jax.ShapeDtypeStruct((1, t...]
    unnamed x2, local copies, waits for them, and re-layouts: 2.25 us -> 1.02 us
where the time goes in v3:
time: 78.7 us; the launch traced here: 78.6 us
  Pallas kernels  77 us (98%)
  local copies, waits for them, and re-layouts  1.02 us (1%)
    pallas_call x1, Pallas kernels, local(): pl.pallas_call(body, name='doremi', out_shape=[jax.ShapeDtypeStruct((1, t...  77 us

profile of v3, /device:TPU:1, one launch (start us, length us, event | category | flops | bytes accessed | tf_op | source)
XLA Modules:
  0.0 78.6 jit_solution(1757368569669609265)
XLA Ops:
  0.6 77.0 %doremi.1 = (f32[1,48]{1,0:T(1,128)S(1)}, f32[1,128]{1,0:T(1,128)S(1)}) custom-call(bf16[48,512]{1,0:T(8,128)(2,1)} %refs_0_.1, bf16[48,512]{1,0:T(8,128)(2,1)} %refs_1_.1, bf16[501,4096]{1,0:T(8,128)(2,1)} %refs_2_.1, bf16[501,4096]{1,0:T(8,128)(2,1)} %refs_3_.1, s32[1,48]{1,0:T(1,128)} %bitcast.8, s32[1,48]{1,0:T(1,128)} %bitcast.9, s32[1,48]{1,0:T(1,128)} %bitcast.10, ...), custom_call_target="tpu_custom_call" | custom-call | flops 12899999744 | bytes 34000000 | tf_op jit(solution)/shard_map/doremi/pallas_call | solution.py:569
  77.6 0.5 copy.12
  78.1 0.5 copy.13

commit v4 on v3

--- a/solution.py
+++ b/solution.py
@@ -24,6 +24,8 @@
 FINE = (0, 1, -1)
 RING4 = (0, 1, -1, 2)
 RING8 = (0, 1, -1, 2, -2, 3, -3, 4)
+PLANE = [(dx, dy) for dx in (2, 1, 3, 0) for dy in (2, 1, 3, 0) if dx or dy]
+PLANE.sort(key=lambda p: -min(p[0], 4 - p[0]) - min(p[1], 4 - p[1]))
 
 
 def ring(add, axis, size, token, need, far, rank, arrival, lag=0.01):
@@ -197,7 +199,7 @@
 def kernel(
     copies, order, rows, tokens,
     ph, rh, pw, rw, tg, dm, kp, pr, out_excess, out_weights,
-    G, W, acc0, acc1, acc2, accC, tgv, dmv, kpv, prv, M0, M1, st, zbuf, ybuf, xbuf, dbuf,
+    G, W, acc0, acc1, acc2, accC, tgv, dmv, kpv, prv, M0, M1, onehot, early, late, zearly, zlate, pearly, plate, dbuf,
     own_sem, small_sem, head_sem, swap_send, swap_recv, g_send, g_recv, m_send, m_recv, s_send, s_recv,
 ):
     x, y, c, z = (lax.axis_index(a) for a in ("dp_0", "dp_1", "dp_2", "tensor"))
@@ -282,11 +284,11 @@
         pltpu.make_async_copy(heads[m], W.at[m, 0], head_sem).start()
 
     barrier = pltpu.get_barrier_semaphore()
-    peers = [peer("z", d) for d in range(1, 8)] + [peer(a, d) for a in "xy" for d in (1, 2, 3)]
-    peers.append({"dp_2": other})
+    peers = [peer(a, d) for a in "xyz" for d in (1, -1)] + [{"dp_2": other}]
     for target in peers:
         pl.semaphore_signal(barrier, inc=1, device_id=target, device_id_type=MESH)
-    st[...] = jnp.zeros_like(st)
+    early[...] = jnp.zeros_like(early)
+    late[...] = jnp.zeros_like(late)
     M0[y] = jnp.zeros((8, 128), jnp.float32)
     with jax.named_scope("entry_barrier"):
         pl.semaphore_wait(barrier, len(peers))
@@ -376,13 +378,13 @@
         acc = accs[group]
         width = acc.shape[-1]
         if group == "C":
-            places = [sub == 4, sub == 5]
+            spots = [jnp.full((8, 128), b, jnp.int32) for b in range(2)]
+            want = [wanted[4 + b : 5 + b, :] for b in range(2)]
         else:
-            places = [
-                sub == jnp.where(lane < 64, at("x", d), at("y", d))
-                for d in {0: (0,), 1: (-1, 1), 2: (2,)}[group]
+            spots = [
+                jnp.where(lane < 64, at("x", d), at("y", d)) for d in {0: (0,), 1: (-1, 1), 2: (2,)}[group]
             ]
-        want = [jnp.sum(jnp.where(p, wanted, 0.0), axis=0, keepdims=True) for p in places]
+            want = [jnp.sum(jnp.where(sub == p, wanted, 0.0), axis=0, keepdims=True) for p in spots]
         want = jnp.concatenate(want, axis=1).astype(jnp.int32) if len(want) > 1 else want[0].astype(jnp.int32)
         vocab = lax.broadcasted_iota(jnp.int32, (rows, width), 0)
         lses, hits = [], []
@@ -399,15 +401,65 @@
                 hit += jnp.sum(jnp.where(match, logits, 0.0), axis=0, keepdims=True)
             lses.append(peak + jnp.log(total))
             hits.append(hit)
-        for k, row in enumerate((lses[0], lses[1], hits[0] - hits[1])):
-            value = st[k]
-            for b, place in enumerate(places):
-                value = jnp.where(place, row[:, 128 * b : 128 * (b + 1)], value)
-            st[k] = value
+        for b, spot in enumerate(spots):
+            one, two, hit = (r[:, 128 * b : 128 * (b + 1)] for r in (lses[0], lses[1], hits[0] - hits[1]))
+            if group == "C":
+                value = jnp.where(sub == spot, one, late[...])
+                value = jnp.where(sub == spot + 2, two, value)
+                late[...] = jnp.where(sub == spot + 4, hit, value)
+            else:
+                value = jnp.where(sub == spot, one, early[0])
+                early[0] = jnp.where(sub == spot + 4, two, value)
+                early[1] = jnp.where(sub == spot, hit, early[1])
+
+    me = x * 4 + y
+    label = lax.broadcasted_iota(jnp.int32, (128, 128), 0).astype(f32)
+
+    def spread_z(buf, value, stage):
+        buf[z] = value
+        for d in (4, 3, 5, 2, 6, 1, 7):
+            pltpu.make_async_remote_copy(
+                src_ref=buf.at[z], dst_ref=buf.at[z], send_sem=s_send.at[stage], recv_sem=s_recv.at[stage],
+                device_id=peer("z", d), device_id_type=MESH,
+            ).start()
+
+    def spread_xy(buf, value, stage):
+        buf[me] = value
+        for dx, dy in PLANE:
+            pltpu.make_async_remote_copy(
+                src_ref=buf.at[me], dst_ref=buf.at[me], send_sem=s_send.at[stage], recv_sem=s_recv.at[stage],
+                device_id={**peer("x", dx), **peer("y", dy)}, device_id_type=MESH,
+            ).start()
+
+    def arrived(buf, stage):
+        wait(buf.at[pl.ds(0, buf.shape[0] - 1)], s_recv.at[stage])
+
+    def joined(parts):
+        peak = parts[0]
+        for p in parts[1:]:
+            peak = jnp.maximum(peak, p)
+        total = jnp.exp(parts[0] - peak)
+        for p in parts[1:]:
+            total = total + jnp.exp(p - peak)
+        return peak + jnp.log(total)
+
+    def added(parts):
+        total = parts[0]
+        for p in parts[1:]:
+            total = total + p
+        return total
+
+    def join_early(buf):
+        n = buf.shape[0]
+        return jnp.stack([joined([buf[s, 0] for s in range(n)]), added([buf[s, 1] for s in range(n)])])
+
+    def join_late(buf):
+        parts = [buf[s] for s in range(buf.shape[0])]
+        return jnp.where(sub < 4, joined(parts), added(parts))
 
     tables = {}
     pending = {g: sum(1 for w in WORK if w[0] == g) for g in accs}
-    steps = 0
+    steps = computes = 0
     for kind, i in order:
         if kind == "send":
             send(i)
@@ -421,17 +473,19 @@
                 for q, dz in enumerate(RING8):
                     for m in (0, 1):
                         swap(m, dz, q)
-                for d in (1, 2, 3):
-                    meta_send("y", d)
             steps += 1
             with jax.named_scope("recv"):
                 receive(i)
         else:
-            if not done_heads:
+            if computes == 0:
+                for d in (1, 2, 3):
+                    meta_send("y", d)
+            if computes == 3:
                 wait(M0.at[pl.ds(0, 3)], m_recv.at[0])
                 M1[x] = M0[...]
                 for d in (1, 2, 3):
                     meta_send("x", d)
+            computes += 1
             with jax.named_scope(f"compute_{i}"):
                 compute(i)
             group = WORK[i][0]
@@ -441,78 +495,61 @@
                     wait(M1.at[pl.ds(0, 3)], m_recv.at[1])
                     for k, name in enumerate(("targets", "domains", "keep")):
                         tables[name] = spread(M1[:, :, k, :].reshape(16, 128))
+                    onehot[...] = jnp.concatenate(
+                        [(tables["domains"][b : b + 1, :] == label).astype(f32) for b in range(6)], axis=1
+                    )
                 with jax.named_scope(f"stats_{group}"):
                     stats(group, tables["targets"])
-
-    def exchange(buf, axis, stage):
-        n, mine = pos[axis][1], pos[axis][0]
-        for d in (4, 3, 5, 2, 6, 1, 7) if n == 8 else (2, 1, 3):
-            pltpu.make_async_remote_copy(
-                src_ref=buf.at[mine], dst_ref=buf.at[mine],
-                send_sem=s_send.at[stage], recv_sem=s_recv.at[stage],
-                device_id=peer(axis, d), device_id_type=MESH,
-            ).start()
-        wait(buf.at[pl.ds(0, n - 1)], s_recv.at[stage])
-        parts = [[buf[s, k] for k in range(3)] for s in range(n)]
-        combined = []
-        for k in (0, 1):
-            peak = parts[0][k]
-            for s in range(1, n):
-                peak = jnp.maximum(peak, parts[s][k])
-            total = jnp.exp(parts[0][k] - peak)
-            for s in range(1, n):
-                total = total + jnp.exp(parts[s][k] - peak)
-            combined.append(peak + jnp.log(total))
-        hit = parts[0][2]
-        for s in range(1, n):
-            hit = hit + parts[s][2]
-        combined.append(hit)
-        return combined
-
-    zbuf[z] = st[...]
-    with jax.named_scope("exchange_z"):
-        result = exchange(zbuf, "z", 0)
-    for k in range(3):
-        ybuf[y, k] = result[k]
-    with jax.named_scope("exchange_y"):
-        result = exchange(ybuf, "y", 1)
-    for k in range(3):
-        xbuf[x, k] = result[k]
-    with jax.named_scope("exchange_x"):
-        lse0, lse1, hit = exchange(xbuf, "x", 2)
+                if group == "C":
+                    spread_z(zlate, late[...], 1)
+                elif not any(pending[g] for g in (0, 1, 2)):
+                    spread_z(zearly, early[...], 0)
 
     keep = tables["keep"]
-    gap = (lse0 - lse1) - hit
-    excess = gap * keep
-    clipped = jnp.maximum(gap, 0.0) * keep
     q = (lane // 16) % 4
-    low = lane % 16
     owner = jnp.where(sub < 4, jnp.where(lane < 64, sub * 4 + q, q * 4 + sub), (2 * (sub - 4) + lane // 64) * 4 + q)
     colour = jnp.where(sub < 4, jnp.where(lane < 64, 0, 1), 2)
-    token = (owner * 2 + c) * 48 + 16 * colour + low
-    batch = token // 512
-    label = lax.broadcasted_iota(jnp.int32, (128, 128), 0).astype(f32)
-    left, right = [], []
-    for b in range(6):
-        bb = batch[b : b + 1, :]
-        top = jnp.where(bb == sub, clipped[b : b + 1, :], 0.0)
-        low_rows = jnp.where(bb == sub - 3, keep[b : b + 1, :], 0.0)
-        left.append(jnp.where(sub < 3, top, low_rows))
-        right.append((tables["domains"][b : b + 1, :] == label).astype(f32))
-    sums = lax.dot_general(
-        jnp.concatenate(left, axis=1), jnp.concatenate(right, axis=1), (((1,), (1,)), ((), ())),
-        precision=lax.Precision.HIGHEST, preferred_element_type=f32,
-    )
+    batch = ((owner * 2 + c) * 48 + 16 * colour + lane % 16) // 512
+
+    def domain_sums(clipped, first, last):
+        left = []
+        for b in range(first, last):
+            bb = batch[b : b + 1, :]
+            top = jnp.where(bb == sub, clipped[b - first : b - first + 1, :], 0.0)
+            low_rows = jnp.where(bb == sub - 3, keep[b : b + 1, :], 0.0)
+            left.append(jnp.where(sub < 3, top, low_rows))
+        return lax.dot_general(
+            jnp.concatenate(left, axis=1), onehot[:, 128 * first : 128 * last], (((1,), (1,)), ((), ())),
+            precision=lax.Precision.HIGHEST, preferred_element_type=f32,
+        )
+
+    with jax.named_scope("exchange_z"):
+        arrived(zearly, 0)
+        spread_xy(pearly, join_early(zearly), 2)
+        with jax.named_scope("late_z"):
+            arrived(zlate, 1)
+        spread_xy(plate, join_late(zlate), 3)
+    with jax.named_scope("exchange_xy"):
+        arrived(pearly, 2)
+        pair = join_early(pearly)
+        gap_early = (pair[0, 0:4] - pair[0, 4:8]) - pair[1, 0:4]
+        sums_early = domain_sums(jnp.maximum(gap_early, 0.0) * keep[0:4], 0, 4)
+        with jax.named_scope("late_xy"):
+            arrived(plate, 3)
+    tile = join_late(plate)
+    gap_late = (tile[0:2] - tile[2:4]) - tile[4:6]
+    sums = sums_early + domain_sums(jnp.maximum(gap_late, 0.0) * keep[4:6], 4, 6)
+    gap = jnp.concatenate([gap_early, gap_late, jnp.zeros((2, 128), f32)], axis=0)
+    excess = gap * keep
     dbuf[c] = sums
 
     def last_copy(slot):
         return pltpu.make_async_remote_copy(
-            src_ref=dbuf.at[slot], dst_ref=dbuf.at[slot], send_sem=s_send.at[3], recv_sem=s_recv.at[3],
+            src_ref=dbuf.at[slot], dst_ref=dbuf.at[slot], send_sem=s_send.at[4], recv_sem=s_recv.at[4],
             device_id={"dp_2": other}, device_id_type=MESH,
         )
 
     last_copy(c).start()
-    me = x * 4 + y
     here = jnp.where((owner == me) & (sub < 6), excess, 0.0)
     j = lax.broadcasted_iota(jnp.int32, (128, 128), 0)
     l = lax.broadcasted_iota(jnp.int32, (128, 128), 1)
@@ -547,9 +584,8 @@
         wait(W.at[:, 1], swap_send)
         wait(M0.at[pl.ds(0, 3)], m_send.at[0])
         wait(M1.at[pl.ds(0, 3)], m_send.at[1])
-        wait(zbuf.at[pl.ds(0, 7)], s_send.at[0])
-        wait(ybuf.at[pl.ds(0, 3)], s_send.at[1])
-        wait(xbuf.at[pl.ds(0, 3)], s_send.at[2])
+        for k, buf in enumerate((zearly, zlate, pearly, plate)):
+            wait(buf.at[pl.ds(0, buf.shape[0] - 1)], s_send.at[k])
         last_copy(c).wait_send()
 
 
@@ -585,14 +621,17 @@
             pltpu.VMEM((1, 128), f32),
             pltpu.VMEM((4, 8, 128), f32),
             pltpu.VMEM((4, 4, 8, 128), f32),
-            pltpu.VMEM((3, 8, 128), f32),
-            pltpu.VMEM((8, 3, 8, 128), f32),
-            pltpu.VMEM((4, 3, 8, 128), f32),
-            pltpu.VMEM((4, 3, 8, 128), f32),
+            pltpu.VMEM((128, 768), f32),
+            pltpu.VMEM((2, 8, 128), f32),
+            pltpu.VMEM((8, 128), f32),
+            pltpu.VMEM((8, 2, 8, 128), f32),
+            pltpu.VMEM((8, 8, 128), f32),
+            pltpu.VMEM((16, 2, 8, 128), f32),
+            pltpu.VMEM((16, 8, 128), f32),
             pltpu.VMEM((2, 8, 128), f32),
             dma, dma((4,)), dma, dma, dma((8,)),
             dma((9,)), dma((arrivals,)),
-            dma((2,)), dma((2,)), dma((4,)), dma((4,)),
+            dma((2,)), dma((2,)), dma((5,)), dma((5,)),
         ],
         compiler_params=pltpu.CompilerParams(
             collective_id=0, has_side_effects=True, vmem_limit_bytes=53 * 1024 * 1024

time: 78.7 us -> 76.1 us (0.967)
  Pallas kernels: 77 us -> 74.4 us
    pallas_call x1, Pallas kernels: 77 us -> 74.4 us  [local(): pl.pallas_call(body, name='doremi', out_shape=[jax.ShapeDtypeStruct((1, t...]
where the time goes in v4:
time: 76.1 us; the launch traced here: 76 us
  Pallas kernels  74.4 us (98%)
  local copies, waits for them, and re-layouts  1.02 us (1%)
    pallas_call x1, Pallas kernels, local(): pl.pallas_call(body, name='doremi', out_shape=[jax.ShapeDtypeStruct((1, t...  74.4 us

profile of v4, /device:TPU:1, one launch (start us, length us, event | category | flops | bytes accessed | tf_op | source)
XLA Modules:
  0.0 76.0 jit_solution(3986125220706503778)
XLA Ops:
  0.6 74.4 %doremi.1 = (f32[1,48]{1,0:T(1,128)S(1)}, f32[1,128]{1,0:T(1,128)S(1)}) custom-call(bf16[48,512]{1,0:T(8,128)(2,1)} %refs_0_.1, bf16[48,512]{1,0:T(8,128)(2,1)} %refs_1_.1, bf16[501,4096]{1,0:T(8,128)(2,1)} %refs_2_.1, bf16[501,4096]{1,0:T(8,128)(2,1)} %refs_3_.1, s32[1,48]{1,0:T(1,128)} %bitcast.8, s32[1,48]{1,0:T(1,128)} %bitcast.9, s32[1,48]{1,0:T(1,128)} %bitcast.10, ...), custom_call_target="tpu_custom_call" | custom-call | flops 12899999744 | bytes 34000000 | tf_op jit(solution)/shard_map/doremi/pallas_call | solution.py:605
  75.0 0.5 copy.12
  75.5 0.5 copy.13

commit v5 on v4

--- a/solution.py
+++ b/solution.py
@@ -12,6 +12,7 @@
 DP_TENSOR = ("dp_0", "dp_1", "dp_2", "tensor")
 AXIS = {"x": "dp_0", "y": "dp_1", "z": "tensor"}
 MESH = pl.DeviceIdType.MESH
+DMA = pltpu.SemaphoreType.DMA
 
 step_size = 1.0
 smoothing = 0.001
@@ -114,7 +115,7 @@
 WORK = [
     (0, (0,)), (0, (1, -1)), (0, (2, -2)), (0, (3, -3, 4)),
     (1, (0,)), (1, (1, -1)), (1, (2, -2)), (1, (3, -3)), (1, (4,)),
-    (2, (0,)), (2, (1, -1)), (2, (2, -2)), (2, (3, -3)), (2, (4,)),
+    (2, (0,)), (2, (1, -1)), (2, (2, -2)), (2, (3,)), (2, (-3,)), (2, (4,)),
     ("C", (0,)), ("C", (1, -1)), ("C", (2, -2)), ("C", (3, -3)), ("C", (4,)),
 ]
 STATS_TIME = {0: 0.34, 1: 0.74, 2: 0.34, "C": 0.74}
@@ -175,7 +176,7 @@
             i = min(ready)
             undone.discard(i)
             order.append(("compute", i))
-            now += 0.25 + 0.54 * len(works[i][1])
+            now += 0.2 + 0.54 * len(works[i][1])
             left[works[i][0]] -= 1
             if not left[works[i][0]]:
                 now += STATS_TIME[works[i][0]]
@@ -200,7 +201,7 @@
     copies, order, rows, tokens,
     ph, rh, pw, rw, tg, dm, kp, pr, out_excess, out_weights,
     G, W, acc0, acc1, acc2, accC, tgv, dmv, kpv, prv, M0, M1, onehot, early, late, zearly, zlate, pearly, plate, dbuf,
-    own_sem, small_sem, head_sem, swap_send, swap_recv, g_send, g_recv, m_send, m_recv, s_send, s_recv,
+    keep_ref, s_send, s_recv,
 ):
     x, y, c, z = (lax.axis_index(a) for a in ("dp_0", "dp_1", "dp_2", "tensor"))
     other = 1 - c
@@ -246,171 +247,12 @@
             return G.at[2, 0, :, at("y", d), :, cs]
         return G.at[2, 1, at("x", d), :, :, cs]
 
-    arrival_at = {}
-    for cp in copies:
-        arrival_at.setdefault(cp["arrival"], [len(arrival_at), 0])[1] += cp["size"]
-    amounts = {
-        32 * KB: G.at[0, :, 0, 0, :, pl.ds(0, 512)],
-        64 * KB: G.at[0, 0, 0, :, :, pl.ds(0, 512)],
-        128 * KB: G.at[0, :, 0, :, :, pl.ds(0, 512)],
-        256 * KB: G.at[0:2, :, 0, :, :, pl.ds(0, 512)],
-    }
-
     def wait(ref, sem):
         pltpu.make_async_copy(ref, ref, sem).wait()
-
-    def send(i):
-        cp = copies[i]
-        ref = view(cp["source"])
-        pltpu.make_async_remote_copy(
-            src_ref=ref, dst_ref=ref,
-            send_sem=g_send.at[SEND_CLASS[cp["source"][:2]]], recv_sem=g_recv.at[arrival_at[cp["arrival"]][0]],
-            device_id=peer(cp["axis"], cp["sign"]), device_id_type=MESH,
-        ).start()
-
-    def receive(arrival):
-        index, size = arrival_at[arrival]
-        wait(amounts[size], g_recv.at[index])
-
-    for m, src in enumerate((ph, rh)):
-        for k in range(3):
-            dst = G.at[k, m, y, x, :, cols(0)] if k == 1 else G.at[k, m, x, y, :, cols(0)]
-            pltpu.make_async_copy(src.at[pl.ds(16 * k, 16), :], dst, own_sem).start()
-    small = ((tg, tgv), (dm, dmv), (kp, kpv), (pr, prv))
-    for k, (src, dst) in enumerate(small):
-        pltpu.make_async_copy(src, dst, small_sem.at[k]).start()
-    heads = (pw, rw)
-    for m in (0, 1):
-        pltpu.make_async_copy(heads[m], W.at[m, 0], head_sem).start()
-
-    barrier = pltpu.get_barrier_semaphore()
-    peers = [peer(a, d) for a in "xyz" for d in (1, -1)] + [{"dp_2": other}]
-    for target in peers:
-        pl.semaphore_signal(barrier, inc=1, device_id=target, device_id_type=MESH)
-    early[...] = jnp.zeros_like(early)
-    late[...] = jnp.zeros_like(late)
-    M0[y] = jnp.zeros((8, 128), jnp.float32)
-    with jax.named_scope("entry_barrier"):
-        pl.semaphore_wait(barrier, len(peers))
-    with jax.named_scope("own_blocks"):
-        wait(G.at[:, :, 0, 0, :, pl.ds(0, 512)], own_sem)
-
-    def meta_send(axis, d):
-        src, dst, k = (M0.at[y], M0.at[y], 0) if axis == "y" else (M0, M1.at[x], 1)
-        pltpu.make_async_remote_copy(
-            src_ref=src, dst_ref=dst, send_sem=m_send.at[k], recv_sem=m_recv.at[k],
-            device_id=peer(axis, d), device_id_type=MESH,
-        ).start()
-
-    def swap(m, dz, q):
-        pltpu.make_async_remote_copy(
-            src_ref=heads[m].at[:, cols(dz)], dst_ref=W.at[m, 1, :, cols(dz)],
-            send_sem=swap_send, recv_sem=swap_recv.at[q],
-            device_id={"dp_2": other}, device_id_type=MESH,
-        ).start()
 
     f32 = jnp.float32
     lane = lax.broadcasted_iota(jnp.int32, (8, 128), 1)
     sub = lax.broadcasted_iota(jnp.int32, (8, 128), 0)
-    accs = {0: acc0, 1: acc1, 2: acc2, "C": accC}
-
-    def block(group, m, dz):
-        cs = cols(dz)
-        if group == "C":
-            return G[2, m, :, :, :, cs].reshape(256, 512)
-        pieces = []
-        for d in {0: (0,), 1: (-1, 1), 2: (2,)}[group]:
-            pieces.append(G[0, m, at("x", d), :, :, cs].reshape(64, 512))
-            pieces.append(G[1, m, at("y", d), :, :, cs].reshape(64, 512))
-        return jnp.concatenate(pieces, axis=0)
-
-    done_heads = set()
-
-    def compute(i):
-        group, dzs = WORK[i]
-        if not done_heads:
-            wait(W.at[:, 0], head_sem)
-        for dz in dzs:
-            if dz not in done_heads:
-                wait(W.at[:, 1, :, cols(dz)], swap_recv.at[RING8.index(dz)])
-                done_heads.add(dz)
-        acc = accs[group]
-        first = 0 in dzs
-
-        for m in (0, 1):
-            rhs = [block(group, m, dz) for dz in dzs]
-            for h in (0, 1):
-                total = None
-                for dz, r in zip(dzs, rhs):
-                    part = lax.dot_general(
-                        W[m, h, :, cols(dz)], r, (((1,), (1,)), ((), ())), preferred_element_type=f32
-                    )
-                    total = part if total is None else total + part
-                acc[m, h] = total if first else acc[m, h] + total
-
-    dev = ((x * 4 + y) * 2 + c) * 8 + z
-    dev_other = ((x * 4 + y) * 2 + other) * 8 + z
-    offsets = (dev * rows, dev_other * rows)
-
-    def spread(quantity):
-        j = lax.broadcasted_iota(jnp.int32, (128, 128), 0)
-        l = lax.broadcasted_iota(jnp.int32, (128, 128), 1)
-        low = l % 16
-        sel_ab = (j == low + jnp.where(l < 64, 0, 16)).astype(f32)
-        sel_c = (j == low + 32).astype(f32)
-        ab = jnp.dot(quantity, sel_ab, precision=lax.Precision.HIGHEST, preferred_element_type=f32)
-        cc = jnp.dot(quantity, sel_c, precision=lax.Precision.HIGHEST, preferred_element_type=f32)
-        d = lax.broadcasted_iota(jnp.int32, (16, 128), 0)
-        l = lax.broadcasted_iota(jnp.int32, (16, 128), 1)
-        q = (l // 16) % 4
-        result = jnp.zeros((8, 128), f32)
-        for a in range(4):
-            owner = jnp.where(l < 64, a * 4 + q, q * 4 + a)
-            row = jnp.sum(jnp.where(d == owner, ab, 0.0), axis=0, keepdims=True)
-            result = jnp.where(sub == a, row, result)
-        for a in range(2):
-            owner = (2 * a + l // 64) * 4 + q
-            row = jnp.sum(jnp.where(d == owner, cc, 0.0), axis=0, keepdims=True)
-            result = jnp.where(sub == 4 + a, row, result)
-        return result
-
-    def stats(group, wanted):
-        acc = accs[group]
-        width = acc.shape[-1]
-        if group == "C":
-            spots = [jnp.full((8, 128), b, jnp.int32) for b in range(2)]
-            want = [wanted[4 + b : 5 + b, :] for b in range(2)]
-        else:
-            spots = [
-                jnp.where(lane < 64, at("x", d), at("y", d)) for d in {0: (0,), 1: (-1, 1), 2: (2,)}[group]
-            ]
-            want = [jnp.sum(jnp.where(sub == p, wanted, 0.0), axis=0, keepdims=True) for p in spots]
-        want = jnp.concatenate(want, axis=1).astype(jnp.int32) if len(want) > 1 else want[0].astype(jnp.int32)
-        vocab = lax.broadcasted_iota(jnp.int32, (rows, width), 0)
-        lses, hits = [], []
-        for m in (0, 1):
-            peak = jnp.maximum(
-                jnp.max(acc[m, 0], axis=0, keepdims=True), jnp.max(acc[m, 1], axis=0, keepdims=True)
-            )
-            total = jnp.zeros((1, width), f32)
-            hit = jnp.zeros((1, width), f32)
-            for h in (0, 1):
-                logits = acc[m, h]
-                total += jnp.sum(jnp.exp(logits - peak), axis=0, keepdims=True)
-                match = vocab == want - offsets[h]
-                hit += jnp.sum(jnp.where(match, logits, 0.0), axis=0, keepdims=True)
-            lses.append(peak + jnp.log(total))
-            hits.append(hit)
-        for b, spot in enumerate(spots):
-            one, two, hit = (r[:, 128 * b : 128 * (b + 1)] for r in (lses[0], lses[1], hits[0] - hits[1]))
-            if group == "C":
-                value = jnp.where(sub == spot, one, late[...])
-                value = jnp.where(sub == spot + 2, two, value)
-                late[...] = jnp.where(sub == spot + 4, hit, value)
-            else:
-                value = jnp.where(sub == spot, one, early[0])
-                early[0] = jnp.where(sub == spot + 4, two, value)
-                early[1] = jnp.where(sub == spot, hit, early[1])
 
     me = x * 4 + y
     label = lax.broadcasted_iota(jnp.int32, (128, 128), 0).astype(f32)
@@ -457,55 +299,234 @@
         parts = [buf[s] for s in range(buf.shape[0])]
         return jnp.where(sub < 4, joined(parts), added(parts))
 
-    tables = {}
-    pending = {g: sum(1 for w in WORK if w[0] == g) for g in accs}
-    steps = computes = 0
-    for kind, i in order:
-        if kind == "send":
-            send(i)
-        elif kind == "recv":
-            if not steps:
-                with jax.named_scope("small_inputs"):
-                    for k, (src, dst) in enumerate(small):
-                        pltpu.make_async_copy(src, dst, small_sem.at[k]).wait()
-                for k, ref in enumerate((tgv, dmv, kpv)):
-                    M0[y, k : k + 1, 0:tokens] = ref[...].astype(f32)
-                for q, dz in enumerate(RING8):
+    def gather(own_sem, small_sem, head_sem, swap_send, swap_recv, g_send, g_recv, m_send, m_recv):
+        arrival_at = {}
+        for cp in copies:
+            arrival_at.setdefault(cp["arrival"], [len(arrival_at), 0])[1] += cp["size"]
+        amounts = {
+            32 * KB: G.at[0, :, 0, 0, :, pl.ds(0, 512)],
+            64 * KB: G.at[0, 0, 0, :, :, pl.ds(0, 512)],
+            128 * KB: G.at[0, :, 0, :, :, pl.ds(0, 512)],
+            256 * KB: G.at[0:2, :, 0, :, :, pl.ds(0, 512)],
+        }
+
+        def send(i):
+            cp = copies[i]
+            ref = view(cp["source"])
+            pltpu.make_async_remote_copy(
+                src_ref=ref, dst_ref=ref,
+                send_sem=g_send.at[SEND_CLASS[cp["source"][:2]]], recv_sem=g_recv.at[arrival_at[cp["arrival"]][0]],
+                device_id=peer(cp["axis"], cp["sign"]), device_id_type=MESH,
+            ).start()
+
+        def receive(arrival):
+            index, size = arrival_at[arrival]
+            wait(amounts[size], g_recv.at[index])
+
+        for m, src in enumerate((ph, rh)):
+            for k in range(3):
+                dst = G.at[k, m, y, x, :, cols(0)] if k == 1 else G.at[k, m, x, y, :, cols(0)]
+                pltpu.make_async_copy(src.at[pl.ds(16 * k, 16), :], dst, own_sem).start()
+        small = ((tg, tgv), (dm, dmv), (kp, kpv), (pr, prv))
+        for k, (src, dst) in enumerate(small):
+            pltpu.make_async_copy(src, dst, small_sem.at[k]).start()
+        heads = (pw, rw)
+
+        barrier = pltpu.get_barrier_semaphore()
+        peers = [peer(a, d) for a in "xyz" for d in (1, -1)] + [{"dp_2": other}]
+        for target in peers:
+            pl.semaphore_signal(barrier, inc=1, device_id=target, device_id_type=MESH)
+        early[...] = jnp.zeros_like(early)
+        late[...] = jnp.zeros_like(late)
+        M0[y] = jnp.zeros((8, 128), jnp.float32)
+        with jax.named_scope("entry_barrier"):
+            pl.semaphore_wait(barrier, len(peers))
+        with jax.named_scope("own_blocks"):
+            wait(G.at[:, :, 0, 0, :, pl.ds(0, 512)], own_sem)
+
+        def meta_send(axis, d):
+            src, dst, k = (M0.at[y], M0.at[y], 0) if axis == "y" else (M0, M1.at[x], 1)
+            pltpu.make_async_remote_copy(
+                src_ref=src, dst_ref=dst, send_sem=m_send.at[k], recv_sem=m_recv.at[k],
+                device_id=peer(axis, d), device_id_type=MESH,
+            ).start()
+
+        def swap(m, dz, q):
+            pltpu.make_async_remote_copy(
+                src_ref=heads[m].at[:, cols(dz)], dst_ref=W.at[m, 1, :, cols(dz)],
+                send_sem=swap_send, recv_sem=swap_recv.at[q],
+                device_id={"dp_2": other}, device_id_type=MESH,
+            ).start()
+
+        accs = {0: acc0, 1: acc1, 2: acc2, "C": accC}
+
+        def block(group, m, dz):
+            cs = cols(dz)
+            if group == "C":
+                return G[2, m, :, :, :, cs].reshape(256, 512)
+            pieces = []
+            for d in {0: (0,), 1: (-1, 1), 2: (2,)}[group]:
+                pieces.append(G[0, m, at("x", d), :, :, cs].reshape(64, 512))
+                pieces.append(G[1, m, at("y", d), :, :, cs].reshape(64, 512))
+            return jnp.concatenate(pieces, axis=0)
+
+        done_heads = set()
+
+        def compute(i):
+            group, dzs = WORK[i]
+            if not done_heads:
+                wait(W.at[:, 0], head_sem)
+            for dz in dzs:
+                if dz not in done_heads:
+                    wait(W.at[:, 1, :, cols(dz)], swap_recv.at[RING8.index(dz)])
+                    done_heads.add(dz)
+            acc = accs[group]
+            first = 0 in dzs
+
+            for m in (0, 1):
+                rhs = [block(group, m, dz) for dz in dzs]
+                for h in (0, 1):
+                    total = None
+                    for dz, r in zip(dzs, rhs):
+                        part = lax.dot_general(
+                            W[m, h, :, cols(dz)], r, (((1,), (1,)), ((), ())), preferred_element_type=f32
+                        )
+                        total = part if total is None else total + part
+                    acc[m, h] = total if first else acc[m, h] + total
+
+        dev = ((x * 4 + y) * 2 + c) * 8 + z
+        dev_other = ((x * 4 + y) * 2 + other) * 8 + z
+        offsets = (dev * rows, dev_other * rows)
+
+        def spread(quantity):
+            j = lax.broadcasted_iota(jnp.int32, (128, 128), 0)
+            l = lax.broadcasted_iota(jnp.int32, (128, 128), 1)
+            low = l % 16
+            sel_ab = (j == low + jnp.where(l < 64, 0, 16)).astype(f32)
+            sel_c = (j == low + 32).astype(f32)
+            ab = jnp.dot(quantity, sel_ab, precision=lax.Precision.HIGHEST, preferred_element_type=f32)
+            cc = jnp.dot(quantity, sel_c, precision=lax.Precision.HIGHEST, preferred_element_type=f32)
+            d = lax.broadcasted_iota(jnp.int32, (16, 128), 0)
+            l = lax.broadcasted_iota(jnp.int32, (16, 128), 1)
+            q = (l // 16) % 4
+            result = jnp.zeros((8, 128), f32)
+            for a in range(4):
+                owner = jnp.where(l < 64, a * 4 + q, q * 4 + a)
+                row = jnp.sum(jnp.where(d == owner, ab, 0.0), axis=0, keepdims=True)
+                result = jnp.where(sub == a, row, result)
+            for a in range(2):
+                owner = (2 * a + l // 64) * 4 + q
+                row = jnp.sum(jnp.where(d == owner, cc, 0.0), axis=0, keepdims=True)
+                result = jnp.where(sub == 4 + a, row, result)
+            return result
+
+        def stats(group, wanted):
+            acc = accs[group]
+            width = acc.shape[-1]
+            if group == "C":
+                spots = [jnp.full((8, 128), b, jnp.int32) for b in range(2)]
+                want = [wanted[4 + b : 5 + b, :] for b in range(2)]
+            else:
+                spots = [
+                    jnp.where(lane < 64, at("x", d), at("y", d)) for d in {0: (0,), 1: (-1, 1), 2: (2,)}[group]
+                ]
+                want = [jnp.sum(jnp.where(sub == p, wanted, 0.0), axis=0, keepdims=True) for p in spots]
+            want = jnp.concatenate(want, axis=1).astype(jnp.int32) if len(want) > 1 else want[0].astype(jnp.int32)
+            vocab = lax.broadcasted_iota(jnp.int32, (rows, width), 0)
+            lses, hits = [], []
+            for m in (0, 1):
+                peak = jnp.maximum(
+                    jnp.max(acc[m, 0], axis=0, keepdims=True), jnp.max(acc[m, 1], axis=0, keepdims=True)
+                )
+                total = jnp.zeros((1, width), f32)
+                hit = jnp.zeros((1, width), f32)
+                for h in (0, 1):
+                    logits = acc[m, h]
+                    total += jnp.sum(jnp.exp(logits - peak), axis=0, keepdims=True)
+                    match = vocab == want - offsets[h]
+                    hit += jnp.sum(jnp.where(match, logits, 0.0), axis=0, keepdims=True)
+                lses.append(peak + jnp.log(total))
+                hits.append(hit)
+            for b, spot in enumerate(spots):
+                one, two, hit = (r[:, 128 * b : 128 * (b + 1)] for r in (lses[0], lses[1], hits[0] - hits[1]))
+                if group == "C":
+                    value = jnp.where(sub == spot, one, late[...])
+                    value = jnp.where(sub == spot + 2, two, value)
+                    late[...] = jnp.where(sub == spot + 4, hit, value)
+                else:
+                    value = jnp.where(sub == spot, one, early[0])
+                    early[0] = jnp.where(sub == spot + 4, two, value)
+                    early[1] = jnp.where(sub == spot, hit, early[1])
+
+        tables = {}
+        pending = {g: sum(1 for w in WORK if w[0] == g) for g in accs}
+        steps = computes = 0
+        for kind, i in order:
+            if kind == "send":
+                send(i)
+            elif kind == "recv":
+                if not steps:
+                    for q, dz in enumerate(RING8):
+                        for m in (0, 1):
+                            swap(m, dz, q)
                     for m in (0, 1):
-                        swap(m, dz, q)
-            steps += 1
-            with jax.named_scope("recv"):
-                receive(i)
-        else:
-            if computes == 0:
-                for d in (1, 2, 3):
-                    meta_send("y", d)
-            if computes == 3:
-                wait(M0.at[pl.ds(0, 3)], m_recv.at[0])
-                M1[x] = M0[...]
-                for d in (1, 2, 3):
-                    meta_send("x", d)
-            computes += 1
-            with jax.named_scope(f"compute_{i}"):
-                compute(i)
-            group = WORK[i][0]
-            pending[group] -= 1
-            if not pending[group]:
-                if not tables:
-                    wait(M1.at[pl.ds(0, 3)], m_recv.at[1])
-                    for k, name in enumerate(("targets", "domains", "keep")):
-                        tables[name] = spread(M1[:, :, k, :].reshape(16, 128))
-                    onehot[...] = jnp.concatenate(
-                        [(tables["domains"][b : b + 1, :] == label).astype(f32) for b in range(6)], axis=1
-                    )
-                with jax.named_scope(f"stats_{group}"):
-                    stats(group, tables["targets"])
-                if group == "C":
-                    spread_z(zlate, late[...], 1)
-                elif not any(pending[g] for g in (0, 1, 2)):
-                    spread_z(zearly, early[...], 0)
-
-    keep = tables["keep"]
+                        pltpu.make_async_copy(heads[m], W.at[m, 0], head_sem).start()
+                    with jax.named_scope("small_inputs"):
+                        for k, (src, dst) in enumerate(small):
+                            pltpu.make_async_copy(src, dst, small_sem.at[k]).wait()
+                    for k, ref in enumerate((tgv, dmv, kpv)):
+                        M0[y, k : k + 1, 0:tokens] = ref[...].astype(f32)
+                steps += 1
+                with jax.named_scope("recv"):
+                    receive(i)
+            else:
+                if computes == 0:
+                    for d in (1, 2, 3):
+                        meta_send("y", d)
+                if computes == 3:
+                    wait(M0.at[pl.ds(0, 3)], m_recv.at[0])
+                    M1[x] = M0[...]
+                    for d in (1, 2, 3):
+                        meta_send("x", d)
+                computes += 1
+                with jax.named_scope(f"compute_{i}"):
+                    compute(i)
+                group = WORK[i][0]
+                pending[group] -= 1
+                if not pending[group]:
+                    if not tables:
+                        wait(M1.at[pl.ds(0, 3)], m_recv.at[1])
+                        for k, name in enumerate(("targets", "domains", "keep")):
+                            tables[name] = spread(M1[:, :, k, :].reshape(16, 128))
+                        onehot[...] = jnp.concatenate(
+                            [(tables["domains"][b : b + 1, :] == label).astype(jnp.bfloat16) for b in range(6)], axis=1
+                        )
+                    with jax.named_scope(f"stats_{group}"):
+                        stats(group, tables["targets"])
+                    if group == "C":
+                        spread_z(zlate, late[...], 1)
+                    elif not any(pending[g] for g in (0, 1, 2)):
+                        spread_z(zearly, early[...], 0)
+
+        keep_ref[...] = tables["keep"]
+        with jax.named_scope("sends_done"):
+            for k in range(2):
+                wait(G.at[k, :, 0, 0, :, pl.ds(0, 7 * 512)], g_send.at[3 * k])
+                wait(G.at[k, :, 0, pl.ds(0, 3)], g_send.at[3 * k + 1])
+                wait(G.at[k, :, pl.ds(0, 3)], g_send.at[3 * k + 2])
+            wait(G.at[2, :, :, :, :, pl.ds(0, 7 * 512)], g_send.at[6])
+            wait(G.at[2, :, pl.ds(0, 3), 0, :, pl.ds(0, 512)], g_send.at[7])
+            wait(G.at[2, :, pl.ds(0, 3), :, :, pl.ds(0, 512)], g_send.at[8])
+            wait(W.at[:, 1], swap_send)
+            wait(M0.at[pl.ds(0, 3)], m_send.at[0])
+            wait(M1.at[pl.ds(0, 3)], m_send.at[1])
+
+    pl.run_scoped(
+        gather, DMA, DMA((4,)), DMA, DMA, DMA((8,)), DMA((9,)),
+        DMA((len({cp["arrival"] for cp in copies}),)), DMA((2,)), DMA((2,)),
+    )
+
+    keep = keep_ref[...]
     q = (lane // 16) % 4
     owner = jnp.where(sub < 4, jnp.where(lane < 64, sub * 4 + q, q * 4 + sub), (2 * (sub - 4) + lane // 64) * 4 + q)
     colour = jnp.where(sub < 4, jnp.where(lane < 64, 0, 1), 2)
@@ -518,10 +539,24 @@
             top = jnp.where(bb == sub, clipped[b - first : b - first + 1, :], 0.0)
             low_rows = jnp.where(bb == sub - 3, keep[b : b + 1, :], 0.0)
             left.append(jnp.where(sub < 3, top, low_rows))
-        return lax.dot_general(
-            jnp.concatenate(left, axis=1), onehot[:, 128 * first : 128 * last], (((1,), (1,)), ((), ())),
-            precision=lax.Precision.HIGHEST, preferred_element_type=f32,
+        left = jnp.concatenate(left, axis=1)
+        thirds = []
+        for _ in range(3):
+            third = left.astype(jnp.bfloat16)
+            thirds.append(third)
+            left = left - third.astype(f32)
+        parts = lax.dot_general(
+            jnp.concatenate(thirds, axis=0), onehot[:, 128 * first : 128 * last], (((1,), (1,)), ((), ())),
+            preferred_element_type=f32,
         )
+        return parts[0:8] + (parts[8:16] + parts[16:24])
+
+    def picked(values, spots):
+        row = jnp.sum(jnp.where(spots, values, 0.0), axis=0, keepdims=True)
+        row = jnp.broadcast_to(row, (8, 128))
+        for shift in (64, 32, 16):
+            row = row + pltpu.roll(row, shift, 1)
+        return row
 
     with jax.named_scope("exchange_z"):
         arrived(zearly, 0)
@@ -534,13 +569,15 @@
         pair = join_early(pearly)
         gap_early = (pair[0, 0:4] - pair[0, 4:8]) - pair[1, 0:4]
         sums_early = domain_sums(jnp.maximum(gap_early, 0.0) * keep[0:4], 0, 4)
+        nothing = jnp.zeros((4, 128), f32)
+        excess = jnp.concatenate([gap_early, nothing], axis=0) * keep
+        mine_a = picked(excess, (owner == me) & (colour == 0))
+        mine_b = picked(excess, (owner == me) & (colour == 1))
         with jax.named_scope("late_xy"):
             arrived(plate, 3)
     tile = join_late(plate)
     gap_late = (tile[0:2] - tile[2:4]) - tile[4:6]
     sums = sums_early + domain_sums(jnp.maximum(gap_late, 0.0) * keep[4:6], 4, 6)
-    gap = jnp.concatenate([gap_early, gap_late, jnp.zeros((2, 128), f32)], axis=0)
-    excess = gap * keep
     dbuf[c] = sums
 
     def last_copy(slot):
@@ -550,17 +587,9 @@
         )
 
     last_copy(c).start()
-    here = jnp.where((owner == me) & (sub < 6), excess, 0.0)
-    j = lax.broadcasted_iota(jnp.int32, (128, 128), 0)
-    l = lax.broadcasted_iota(jnp.int32, (128, 128), 1)
-    sel_ab = (j == l % 16 + jnp.where(l < 64, 0, 16)).astype(f32)
-    sel_c = (j == l % 16 + 32).astype(f32)
-    spots = jnp.concatenate([jnp.where(sub < 4, here, 0.0), jnp.where(sub >= 4, here, 0.0)], axis=1)
-    mine_out = lax.dot_general(
-        spots, jnp.concatenate([sel_ab, sel_c], axis=1), (((1,), (1,)), ((), ())),
-        precision=lax.Precision.HIGHEST, preferred_element_type=f32,
-    )
-    mine_row = jnp.sum(mine_out, axis=0, keepdims=True)
+    excess = jnp.concatenate([nothing, gap_late, nothing[0:2]], axis=0) * keep
+    mine_c = picked(excess, (owner == me) & (colour == 2) & (sub < 6))
+    mine_row = jnp.where(lane < 16, mine_a, jnp.where(lane < 32, mine_b, mine_c))[0:1, :]
     prior = prv[...]
     weights = prior / jnp.sum(prior, axis=1, keepdims=True)
     with jax.named_scope("partner_sums"):
@@ -574,16 +603,6 @@
     out_excess[...] = mine_row[:, 0:tokens]
 
     with jax.named_scope("sends_done"):
-        for k in range(2):
-            wait(G.at[k, :, 0, 0, :, pl.ds(0, 7 * 512)], g_send.at[3 * k])
-            wait(G.at[k, :, 0, pl.ds(0, 3)], g_send.at[3 * k + 1])
-            wait(G.at[k, :, pl.ds(0, 3)], g_send.at[3 * k + 2])
-        wait(G.at[2, :, :, :, :, pl.ds(0, 7 * 512)], g_send.at[6])
-        wait(G.at[2, :, pl.ds(0, 3), 0, :, pl.ds(0, 512)], g_send.at[7])
-        wait(G.at[2, :, pl.ds(0, 3), :, :, pl.ds(0, 512)], g_send.at[8])
-        wait(W.at[:, 1], swap_send)
-        wait(M0.at[pl.ds(0, 3)], m_send.at[0])
-        wait(M1.at[pl.ds(0, 3)], m_send.at[1])
         for k, buf in enumerate((zearly, zlate, pearly, plate)):
             wait(buf.at[pl.ds(0, buf.shape[0] - 1)], s_send.at[k])
         last_copy(c).wait_send()
@@ -593,9 +612,7 @@
     rows, tokens = pw.shape[0], targets.shape[0]
     copies = gather_plan()
     order = schedule(copies, WORK)
-    arrivals = len({c["arrival"] for c in copies})
     f32, bf16 = jnp.float32, jnp.bfloat16
-    dma = pltpu.SemaphoreType.DMA
     anywhere = pl.BlockSpec(memory_space=pltpu.HBM)
     inside = pl.BlockSpec(memory_space=pltpu.VMEM)
 
@@ -621,7 +638,7 @@
             pltpu.VMEM((1, 128), f32),
             pltpu.VMEM((4, 8, 128), f32),
             pltpu.VMEM((4, 4, 8, 128), f32),
-            pltpu.VMEM((128, 768), f32),
+            pltpu.VMEM((128, 768), bf16),
             pltpu.VMEM((2, 8, 128), f32),
             pltpu.VMEM((8, 128), f32),
             pltpu.VMEM((8, 2, 8, 128), f32),
@@ -629,9 +646,8 @@
             pltpu.VMEM((16, 2, 8, 128), f32),
             pltpu.VMEM((16, 8, 128), f32),
             pltpu.VMEM((2, 8, 128), f32),
-            dma, dma((4,)), dma, dma, dma((8,)),
-            dma((9,)), dma((arrivals,)),
-            dma((2,)), dma((2,)), dma((5,)), dma((5,)),
+            pltpu.VMEM((8, 128), f32),
+            DMA((5,)), DMA((5,)),
         ],
         compiler_params=pltpu.CompilerParams(
             collective_id=0, has_side_effects=True, vmem_limit_bytes=53 * 1024 * 1024

time: 76.1 us -> 73.1 us (0.961)
  Pallas kernels: 74.4 us -> 71.3 us
    pallas_call x1, Pallas kernels: 74.4 us -> 71.3 us  [local(): pl.pallas_call(body, name='doremi', out_shape=[jax.ShapeDtypeStruct((1, t...]
where the time goes in v5:
time: 73.1 us; the launch traced here: 73 us
  Pallas kernels  71.3 us (98%)
  local copies, waits for them, and re-layouts  1.02 us (1%)
    pallas_call x1, Pallas kernels, local(): pl.pallas_call(body, name='doremi', out_shape=[jax.ShapeDtypeStruct((1, t...  71.3 us

profile of v5, /device:TPU:1, one launch (start us, length us, event | category | flops | bytes accessed | tf_op | source)
XLA Modules:
  0.0 73.0 jit_solution(14003699043775437620)
XLA Ops:
  0.6 71.3 %doremi.1 = (f32[1,48]{1,0:T(1,128)S(1)}, f32[1,128]{1,0:T(1,128)S(1)}) custom-call(bf16[48,512]{1,0:T(8,128)(2,1)} %refs_0_.1, bf16[48,512]{1,0:T(8,128)(2,1)} %refs_1_.1, bf16[501,4096]{1,0:T(8,128)(2,1)} %refs_2_.1, bf16[501,4096]{1,0:T(8,128)(2,1)} %refs_3_.1, s32[1,48]{1,0:T(1,128)} %bitcast.8, s32[1,48]{1,0:T(1,128)} %bitcast.9, s32[1,48]{1,0:T(1,128)} %bitcast.10, ...), custom_call_target="tpu_custom_call" | custom-call | flops 12899999744 | bytes 34000000 | tf_op jit(solution)/shard_map/doremi/pallas_call | solution.py:622
  71.9 0.5 copy.12
  72.4 0.5 copy.13

commit v6 on v5

--- a/solution.py
+++ b/solution.py
@@ -23,6 +23,8 @@
 BACKLOG = 1.5
 LAG = 0.6
 FINE = (0, 1, -1)
+AHEAD = 20
+CHECKPOINTS = range(140, 470, 10)
 RING4 = (0, 1, -1, 2)
 RING8 = (0, 1, -1, 2, -2, 3, -3, 4)
 PLANE = [(dx, dy) for dx in (2, 1, 3, 0) for dy in (2, 1, 3, 0) if dx or dy]
@@ -299,7 +301,7 @@
         parts = [buf[s] for s in range(buf.shape[0])]
         return jnp.where(sub < 4, joined(parts), added(parts))
 
-    def gather(own_sem, small_sem, head_sem, swap_send, swap_recv, g_send, g_recv, m_send, m_recv):
+    def gather(own_sem, small_sem, head_sem, swap_send, swap_recv, g_send, g_recv, m_send, m_recv, pace):
         arrival_at = {}
         for cp in copies:
             arrival_at.setdefault(cp["arrival"], [len(arrival_at), 0])[1] += cp["size"]
@@ -461,7 +463,16 @@
         tables = {}
         pending = {g: sum(1 for w in WORK if w[0] == g) for g in accs}
         steps = computes = 0
-        for kind, i in order:
+        assert CHECKPOINTS[-1] < len(order)
+        for position, (kind, i) in enumerate(order):
+            if position in CHECKPOINTS:
+                @pl.when(c == 0)
+                def _():
+                    pl.semaphore_signal(pace, inc=1, device_id={"dp_2": other}, device_id_type=MESH)
+            if position + AHEAD in CHECKPOINTS:
+                @pl.when(c == 1)
+                def _():
+                    pl.semaphore_wait(pace, 1)
             if kind == "send":
                 send(i)
             elif kind == "recv":
@@ -523,7 +534,7 @@
 
     pl.run_scoped(
         gather, DMA, DMA((4,)), DMA, DMA, DMA((8,)), DMA((9,)),
-        DMA((len({cp["arrival"] for cp in copies}),)), DMA((2,)), DMA((2,)),
+        DMA((len({cp["arrival"] for cp in copies}),)), DMA((2,)), DMA((2,)), pltpu.SemaphoreType.REGULAR,
     )
 
     keep = keep_ref[...]

time: 73.1 us -> 71.7 us (0.981)
  Pallas kernels: 71.3 us -> 69.9 us
    pallas_call x1, Pallas kernels: 71.3 us -> 69.9 us  [local(): pl.pallas_call(body, name='doremi', out_shape=[jax.ShapeDtypeStruct((1, t...]
where the time goes in v6:
time: 71.7 us; the launch traced here: 71.6 us
  Pallas kernels  69.9 us (97%)
  local copies, waits for them, and re-layouts  1.02 us (1%)
    pallas_call x1, Pallas kernels, local(): pl.pallas_call(body, name='doremi', out_shape=[jax.ShapeDtypeStruct((1, t...  69.9 us

profile of v6, /device:TPU:1, one launch (start us, length us, event | category | flops | bytes accessed | tf_op | source)
XLA Modules:
  0.0 71.6 jit_solution(15641100328237546150)
XLA Ops:
  0.6 69.9 %doremi.1 = (f32[1,48]{1,0:T(1,128)S(1)}, f32[1,128]{1,0:T(1,128)S(1)}) custom-call(bf16[48,512]{1,0:T(8,128)(2,1)} %refs_0_.1, bf16[48,512]{1,0:T(8,128)(2,1)} %refs_1_.1, bf16[501,4096]{1,0:T(8,128)(2,1)} %refs_2_.1, bf16[501,4096]{1,0:T(8,128)(2,1)} %refs_3_.1, s32[1,48]{1,0:T(1,128)} %bitcast.8, s32[1,48]{1,0:T(1,128)} %bitcast.9, s32[1,48]{1,0:T(1,128)} %bitcast.10, ...), custom_call_target="tpu_custom_call" | custom-call | flops 12899999744 | bytes 34000000 | tf_op jit(solution)/shard_map/doremi/pallas_call | solution.py:633
  70.6 0.5 copy.12
  71.1 0.5 copy.13

commit v7 on v6

--- a/solution.py
+++ b/solution.py
@@ -24,7 +24,7 @@
 LAG = 0.6
 FINE = (0, 1, -1)
 AHEAD = 20
-CHECKPOINTS = range(140, 470, 10)
+CHECKPOINTS = range(140, 400, 10)
 RING4 = (0, 1, -1, 2)
 RING8 = (0, 1, -1, 2, -2, 3, -3, 4)
 PLANE = [(dx, dy) for dx in (2, 1, 3, 0) for dy in (2, 1, 3, 0) if dx or dy]

time: 71.7 us -> 71.8 us (level)
  no operation moved by 1% of the time
where the time goes in v7:
time: 71.8 us; the launch traced here: 71.6 us
  Pallas kernels  70 us (97%)
  local copies, waits for them, and re-layouts  1.02 us (1%)
    pallas_call x1, Pallas kernels, local(): pl.pallas_call(body, name='doremi', out_shape=[jax.ShapeDtypeStruct((1, t...  70 us

profile of v7, /device:TPU:1, one launch (start us, length us, event | category | flops | bytes accessed | tf_op | source)
XLA Modules:
  0.0 71.6 jit_solution(6678623014754916498)
XLA Ops:
  0.6 70.0 %doremi.1 = (f32[1,48]{1,0:T(1,128)S(1)}, f32[1,128]{1,0:T(1,128)S(1)}) custom-call(bf16[48,512]{1,0:T(8,128)(2,1)} %refs_0_.1, bf16[48,512]{1,0:T(8,128)(2,1)} %refs_1_.1, bf16[501,4096]{1,0:T(8,128)(2,1)} %refs_2_.1, bf16[501,4096]{1,0:T(8,128)(2,1)} %refs_3_.1, s32[1,48]{1,0:T(1,128)} %bitcast.8, s32[1,48]{1,0:T(1,128)} %bitcast.9, s32[1,48]{1,0:T(1,128)} %bitcast.10, ...), custom_call_target="tpu_custom_call" | custom-call | flops 12899999744 | bytes 34000000 | tf_op jit(solution)/shard_map/doremi/pallas_call | solution.py:633
  70.6 0.5 copy.12
  71.1 0.5 copy.13
